TPU v7x, 32 devices: a whole 2x2x4 slice. The times are simulated.
32 devices in a mesh: dp: 8 (over z, x), rep: 4 (over y, core).
Axes of the slice: x: 2, y: 2, z: 4, core: 2. Of those that a mesh axis runs over, the one named last changes fastest.
Arguments:
- tokens: bfloat16 [8192, 2048], P(('rep', 'dp')), parts along dimension 0, may hold values from -12 to 12
- router: bfloat16 [8192, 8], P('rep'), parts along dimension 0, may hold values from -12 to 12
- w_gate: bfloat16 [8, 2048, 768], P('dp'), may hold values from -0.125 to 0.125
- w_up: bfloat16 [8, 2048, 768], P('dp'), may hold values from -0.125 to 0.125
- w_down: bfloat16 [8, 768, 2048], P('dp'), may hold values from -0.21875 to 0.21875
- picks: int32 [32, 32], P(('rep', 'dp')), parts along dimension 0, may hold values from 0 to 2047, as said below
Outputs:
- combined: bfloat16 [8192, 2048], P(('rep', 'dp')), parts along dimension 0
There are 4 independent parts, one for each index of `rep`. A program takes and returns all parts, laid end to end along the dimension named above; an argument that names none is the same for every part. Nothing has to cross between parts.
Inputs may be any that keep to these rules, and one draw needn't show every extreme that they name: `picks`: row e holds 32 different tokens taken by expert e, sorted by the device that holds them (256 tokens each, in order); at most 6 of them lie among one device's tokens, and in every row exactly 6 lie among some device's tokens.
All inputs are finite; a program needn't handle non-finite values.
Results may differ from a plain program's by a relative error of at most 0.0062.
Values may be sent and summed in bfloat16 or wider, within the bound.
No kernel may reach another device: no remote copies, remote signals or barrier semaphores. Data moves between devices by JAX's collectives and lax.ppermute only.
A program may use at most 64 MiB of HBM per device.

v0:
```python
import jax
import jax.numpy as jnp
from jax import lax
from jax.sharding import PartitionSpec as P

MOST = 6


def feed_forward(buffer_rows, gate_values, gate_w, up_w, down_w):
    gate_act = jnp.dot(buffer_rows, gate_w, preferred_element_type=jnp.float32)
    up_act = jnp.dot(buffer_rows, up_w, preferred_element_type=jnp.float32)
    hidden = (gate_values.astype(jnp.float32)[:, None] * jax.nn.silu(gate_act) * up_act).astype(
        jnp.bfloat16
    )
    return jnp.dot(hidden, down_w, preferred_element_type=jnp.float32).astype(jnp.bfloat16)


def body(tokens, router, w_gate, w_up, w_down, picks):
    sources = lax.axis_size("dp")
    tok_dev = tokens.shape[0]
    width = tokens.shape[1]
    experts = router.shape[1]
    my_picks = picks[0]
    capacity = my_picks.shape[0]
    logits = jnp.dot(tokens, router, preferred_element_type=jnp.float32)
    shares = jax.nn.softmax(logits, axis=1)
    source_of = my_picks // tok_dev
    block_ids = jnp.arange(sources, dtype=jnp.int32)
    counts = jnp.sum((source_of[None, :] == block_ids[:, None]).astype(jnp.int32), axis=1)
    starts = jnp.cumsum(counts) - counts
    slot_pos = jnp.arange(MOST, dtype=jnp.int32)
    within = jnp.arange(capacity, dtype=jnp.int32) - starts[source_of]
    flat_index = source_of * MOST + within
    position = jnp.clip(starts[:, None] + slot_pos[None, :], 0, capacity - 1)
    to_owner = jnp.where(
        slot_pos[None, :] < counts[:, None], my_picks[position] - block_ids[:, None] * tok_dev, -1
    )
    local_index = lax.all_to_all(to_owner, "dp", split_axis=0, concat_axis=0, tiled=True)
    live_slot = local_index >= 0
    safe_index = jnp.maximum(local_index, 0)
    send_rows = jnp.where(live_slot[:, :, None], tokens[safe_index], jnp.zeros((), tokens.dtype))
    columns = lax.all_to_all(
        shares.T.astype(jnp.bfloat16), "dp", split_axis=0, concat_axis=1, tiled=True
    ).astype(jnp.float32)
    gate_dense = (experts * columns[0][my_picks]).astype(jnp.bfloat16)
    received = lax.all_to_all(send_rows, "dp", split_axis=0, concat_axis=0, tiled=True)
    gate_flat = jnp.zeros((sources * MOST,), jnp.bfloat16).at[flat_index].set(gate_dense)
    buffer_rows = received.reshape(sources * MOST, width)
    expert_out = feed_forward(buffer_rows, gate_flat, w_gate[0], w_up[0], w_down[0])
    returned = lax.all_to_all(
        expert_out.reshape(sources, MOST, width), "dp", split_axis=0, concat_axis=0, tiled=True
    )
    onehot = (local_index.reshape(1, -1) == jnp.arange(tok_dev, dtype=jnp.int32)[:, None]).astype(
        jnp.bfloat16
    )
    combined = jnp.dot(
        onehot, returned.reshape(sources * MOST, width), preferred_element_type=jnp.float32
    )
    return combined.astype(jnp.bfloat16)


def solution(mesh):
    return jax.shard_map(
        body,
        mesh=mesh,
        in_specs=(
            P(("rep", "dp"), None),
            P("rep", None),
            P("dp", None, None),
            P("dp", None, None),
            P("dp", None, None),
            P(("rep", "dp"), None),
        ),
        out_specs=P(("rep", "dp"), None),
        check_vma=False,
    )
```

profile of v0, /device:TPU:0, one launch (start us, length us, event | category | flops | bytes accessed | tf_op | source)
XLA Modules:
  0.0 63.1 jit_solution(9098866142192156870)
XLA Ops:
  0.0 0.8 %fusion.32 = s32[32]{0:T(128)S(1)} fusion(s32[1,32]{1,0:T(1,128)} %param.11), kind=kLoop, calls=%fused_computation.61 | loop fusion | flops 480 | bytes 256 | tf_op jit(solution)/shard_map/eq | solution.py:29
  1.3 1.4 %gather_fusion = s32[48]{0:T(128)S(1)} fusion(s32[32]{0:T(128)} %bitcast.65, s32[1024]{0:T(1024)S(1)} %pad_clamp_fusion.3), kind=kCustom, calls=%fused_computation | custom fusion | bytes 576 | tf_op jit(solution)/shard_map/gather | solution.py:36
  3.5 7.3 %all-to-all-start = ((s32[8,1,6]{2,1,0:T(1,128)}), s32[8,1,6]{2,1,0:T(1,128)S(1)}, u32[]{:S(2)}, u32[]{:S(2)}) async-start(s32[8,1,6]{2,1,0:T(1,128)} %bitcast.4), calls=%async_computation | async-start | bytes 8192 | tf_op jit(solution)/shard_map/all_to_all | solution.py:38
  10.8 1.6 %fusion.36 = (f32[256]{0:T(256)S(1)}, f32[256,8]{0,1:T(8,128)S(1)}) fusion(bf16[256,2048]{1,0:T(8,128)(2,1)} %param.6, bf16[2048,8]{0,1:T(8,128)(2,1)S(1)} %copy-done.2), kind=kOutput, calls=%fused_computation.65 | convolution fusion | flops 8390400 | bytes 1090560 | tf_op jit(solution)/shard_map/dot_general | solution.py:25
  12.5 0.7 %gather_fusion.1 = s32[32]{0:T(128)S(1)} fusion(s32[8]{0:T(128)S(1)} %bitcast_subtract_fusion.1, s32[1024]{0:T(1024)S(1)} %get-tuple-element.11), kind=kCustom, calls=%fused_computation.1 | custom fusion | bytes 384 | tf_op jit(solution)/shard_map/gather | solution.py:32
  15.1 2.1 %all-to-all-done = s32[8,1,6]{2,1,0:T(1,128)S(1)} async-done(((s32[8,1,6]{2,1,0:T(1,128)}), s32[8,1,6]{2,1,0:T(1,128)S(1)}, u32[]{:S(2)}, u32[]{:S(2)}) %all-to-all-start) | async-done | bytes 224 | tf_op jit(solution)/shard_map/all_to_all | solution.py:38
  17.2 3.9 %all-to-all-start.1 = ((bf16[8,2,128]{2,1,0:T(2,128)(2,1)}), bf16[8,2,128]{2,1,0:T(2,128)(2,1)S(1)}, u32[]{:S(2)}, u32[]{:S(2)}) async-start(bf16[8,2,128]{2,1,0:T(2,128)(2,1)} %reshape.372), calls=%async_computation.1 | async-start | bytes 8192 | tf_op jit(solution)/shard_map/all_to_all | solution.py:42
  21.2 2.2 %gather_fusion.3 = bf16[48,2048]{1,0:T(8,128)(2,1)S(1)} fusion(bf16[256,2048]{1,0:T(8,128)(2,1)} %param.6, s32[1024]{0:T(1024)S(1)} %pad_clamp_fusion), kind=kCustom, calls=%fused_computation.3 | custom fusion | bytes 393408 | tf_op jit(solution)/shard_map/gather | solution.py:41
  23.5 0.8 %reshape.342 = bf16[8,6,2048]{2,1,0:T(8,128)(2,1)} reshape(bf16[48,2048]{1,0:T(8,128)(2,1)S(1)} %gather_fusion.3) | data formatting | bytes 393216 | tf_op jit(solution)/shard_map/gather | solution.py:41
  24.2 1.7 %broadcast_select_fusion = bf16[8,6,2048]{2,1,0:T(8,128)(2,1)} fusion(bf16[8,6,2048]{2,1,0:T(8,128)(2,1)} %reshape.342, pred[8,6]{1,0:T(8,128)(4,1)S(1)} %compare_bitcast_fusion), kind=kLoop, calls=%fused_computation.15 | loop fusion | flops 98304 | bytes 393264 | tf_op jit(solution)/shard_map/jit(_where)/select_n | solution.py:41
  26.0 1.6 %all-to-all-done.1 = bf16[8,2,128]{2,1,0:T(2,128)(2,1)S(1)} async-done(((bf16[8,2,128]{2,1,0:T(2,128)(2,1)}), bf16[8,2,128]{2,1,0:T(2,128)(2,1)S(1)}, u32[]{:S(2)}, u32[]{:S(2)}) %all-to-all-start.1) | async-done | bytes 4128 | tf_op jit(solution)/shard_map/all_to_all | solution.py:42
  27.6 4.4 %all-to-all-start.2 = ((bf16[8,6,2048]{2,1,0:T(8,128)(2,1)}), bf16[8,6,2048]{2,1,0:T(8,128)(2,1)}, u32[]{:S(2)}, u32[]{:S(2)}) async-start(bf16[8,6,2048]{2,1,0:T(8,128)(2,1)} %broadcast_select_fusion), calls=%async_computation.2 | async-start | bytes 524288 | tf_op jit(solution)/shard_map/all_to_all | solution.py:46
  32.0 0.7 %gather_fusion.2 = f32[32]{0:T(128)S(1)} fusion(f32[2048]{0:T(1024)S(1)} %bitcast.66, s32[1024]{0:T(1024)S(1)} %get-tuple-element.10), kind=kCustom, calls=%fused_computation.2 | custom fusion | bytes 384 | tf_op jit(solution)/shard_map/gather | solution.py:45
  32.7 0.8 %scatter_custom_fusion = bf16[48]{0:T(256)(128)(2,1)S(1)} fusion(s32[32]{0:T(128)S(1)} %fusion.30, bf16[32]{0:T(256)(128)(2,1)S(1)} %multiply_convert_fusion, bf16[]{:T(256)} %constant.14.clone.1), kind=kCustom, calls=%fused_computation.62 | custom fusion | bytes 98 | tf_op jit(solution)/shard_map/scatter | solution.py:47
  33.5 6.8 %all-to-all-done.2 = bf16[8,6,2048]{2,1,0:T(8,128)(2,1)} async-done(((bf16[8,6,2048]{2,1,0:T(8,128)(2,1)}), bf16[8,6,2048]{2,1,0:T(8,128)(2,1)}, u32[]{:S(2)}, u32[]{:S(2)}) %all-to-all-start.2) | async-done | bytes 196640 | tf_op jit(solution)/shard_map/all_to_all | solution.py:46
  40.3 1.0 %reshape.313 = bf16[48,2048]{1,0:T(8,128)(2,1)S(1)} reshape(bf16[8,6,2048]{2,1,0:T(8,128)(2,1)} %all-to-all-done.2) | data formatting | bytes 393216 | tf_op jit(solution)/shard_map/reshape | solution.py:48
  41.3 3.2 %fusion.4 = f32[48,768]{1,0:T(8,128)} fusion(bf16[48,2048]{1,0:T(8,128)(2,1)S(1)} %reshape.313, bf16[1,2048,768]{2,1,0:T(8,128)(2,1)} %param.8), kind=kOutput, calls=%fused_computation.9 | convolution fusion | flops 150994944 | bytes 3489792 | tf_op jit(solution)/shard_map/dot_general | solution.py:10
  44.5 3.2 %fusion.6 = bf16[48,2048]{1,0:T(8,128)(2,1)S(1)} fusion(bf16[1,768,2048]{2,1,0:T(8,128)(2,1)S(1)} %copy-done, bf16[48,2048]{1,0:T(8,128)(2,1)S(1)} %reshape.313, bf16[1,2048,768]{2,1,0:T(8,128)(2,1)} %param.9, f32[48,768]{1,0:T(8,128)} %fusion.4, f32[48]{0:T(128)S(1)} %convert_element_type.40), kind=kOutput, calls=%fused_computation.12 | convolution fusion | flops 302346240 | bytes 6832320 | tf_op jit(solution)/shard_map/dot_general | solution.py:15
  47.7 0.8 %reshape.314 = bf16[8,6,2048]{2,1,0:T(8,128)(2,1)} reshape(bf16[48,2048]{1,0:T(8,128)(2,1)S(1)} %fusion.6) | data formatting | bytes 393216 | tf_op jit(solution)/shard_map/reshape | solution.py:51
  48.5 3.4 %all-to-all-start.3 = ((bf16[8,6,2048]{2,1,0:T(8,128)(2,1)}), bf16[8,6,2048]{2,1,0:T(8,128)(2,1)S(1)}, u32[]{:S(2)}, u32[]{:S(2)}) async-start(bf16[8,6,2048]{2,1,0:T(8,128)(2,1)} %reshape.314), calls=%async_computation.3 | async-start | bytes 524288 | tf_op jit(solution)/shard_map/all_to_all | solution.py:50
  52.5 0.7 %reduce.3 = s32[8,6]{1,0:T(8,128)S(1)} reduce(s32[8,1,6]{2,1,0:T(1,128)S(1)} %all-to-all-done, s32[]{:T(128)} %broadcast.285), dimensions={1}, to_apply=%all_to_all.20.reduce_sub_computation.3 | reduce | bytes 388 | tf_op jit(solution)/shard_map/all_to_all | solution.py:38
  53.3 6.8 %all-to-all-done.3 = bf16[8,6,2048]{2,1,0:T(8,128)(2,1)S(1)} async-done(((bf16[8,6,2048]{2,1,0:T(8,128)(2,1)}), bf16[8,6,2048]{2,1,0:T(8,128)(2,1)S(1)}, u32[]{:S(2)}, u32[]{:S(2)}) %all-to-all-start.3) | async-done | bytes 196640 | tf_op jit(solution)/shard_map/all_to_all | solution.py:50
  60.1 0.7 %reshape.315 = bf16[48,2048]{1,0:T(8,128)(2,1)} reshape(bf16[8,6,2048]{2,1,0:T(8,128)(2,1)S(1)} %all-to-all-done.3) | data formatting | bytes 393216 | tf_op jit(solution)/shard_map/reshape | solution.py:57
  60.8 2.3 %convolution_convert_fusion = bf16[256,2048]{1,0:T(8,128)(2,1)} fusion(bf16[48,2048]{1,0:T(8,128)(2,1)} %reshape.315, s32[48]{0:T(128)S(1)} %eq.34), kind=kOutput, calls=%fused_computation.11 | convolution fusion | flops 50868224 | bytes 1245376 | tf_op jit(solution)/shard_map/dot_general | solution.py:56
  (33 shorter events, 4.0 us)
Async XLA Ops:
  0.0 44.5 %copy-start = (bf16[1,768,2048]{2,1,0:T(8,128)(2,1)S(1)}, bf16[1,768,2048]{2,1,0:T(8,128)(2,1)}, u32[]{:S(2)}) copy-start(bf16[1,768,2048]{2,1,0:T(8,128)(2,1)} %param.10) | copy-start | bytes 9437188
  0.0 10.8 %copy-start.1 = (s32[1,32]{1,0:T(1,128)S(1)}, s32[1,32]{1,0:T(1,128)}, u32[]{:S(2)}) copy-start(s32[1,32]{1,0:T(1,128)} %param.11) | copy-start | bytes 388
  0.0 10.8 %copy-start.2 = (bf16[2048,8]{0,1:T(8,128)(2,1)S(1)}, bf16[2048,8]{0,1:T(8,128)(2,1)}, u32[]{:S(2)}) copy-start(bf16[2048,8]{0,1:T(8,128)(2,1)} %param.7) | copy-start | bytes 98308
  3.5 13.7 %all-to-all-start = ((s32[8,1,6]{2,1,0:T(1,128)}), s32[8,1,6]{2,1,0:T(1,128)S(1)}, u32[]{:S(2)}, u32[]{:S(2)}) async-start(s32[8,1,6]{2,1,0:T(1,128)} %bitcast.4), calls=%async_computation | async-start | bytes 8192 | tf_op jit(solution)/shard_map/all_to_all | solution.py:38
  17.2 10.4 %all-to-all-start.1 = ((bf16[8,2,128]{2,1,0:T(2,128)(2,1)}), bf16[8,2,128]{2,1,0:T(2,128)(2,1)S(1)}, u32[]{:S(2)}, u32[]{:S(2)}) async-start(bf16[8,2,128]{2,1,0:T(2,128)(2,1)} %reshape.372), calls=%async_computation.1 | async-start | bytes 8192 | tf_op jit(solution)/shard_map/all_to_all | solution.py:42
  27.6 12.7 %all-to-all-start.2 = ((bf16[8,6,2048]{2,1,0:T(8,128)(2,1)}), bf16[8,6,2048]{2,1,0:T(8,128)(2,1)}, u32[]{:S(2)}, u32[]{:S(2)}) async-start(bf16[8,6,2048]{2,1,0:T(8,128)(2,1)} %broadcast_select_fusion), calls=%async_computation.2 | async-start | bytes 524288 | tf_op jit(solution)/shard_map/all_to_all | solution.py:46
  48.5 11.6 %all-to-all-start.3 = ((bf16[8,6,2048]{2,1,0:T(8,128)(2,1)}), bf16[8,6,2048]{2,1,0:T(8,128)(2,1)S(1)}, u32[]{:S(2)}, u32[]{:S(2)}) async-start(bf16[8,6,2048]{2,1,0:T(8,128)(2,1)} %reshape.314), calls=%async_computation.3 | async-start | bytes 524288 | tf_op jit(solution)/shard_map/all_to_all | solution.py:50
where the time goes:
time: 63.7 us; the launch traced here: 63.1 us
  starting transfers between devices  19 us (30%)
  waiting for transfers between devices  17.3 us (27%)
  local copies, waits for them, and re-layouts  11.3 us (18%)
  matrix products  10.3 us (16%)
  other arithmetic  5.13 us (8%)
    all_to_all x1, starting transfers between devices, body(): lax.all_to_all(to_owner, 'dp', split_axis=0, concat_axis=0, tiled=True)  7.29 us
    all_to_all x1, waiting for transfers between devices, body(): lax.all_to_all(send_rows, 'dp', split_axis=0, concat_axis=0, tiled=True)  6.8 us
    all_to_all x1, waiting for transfers between devices, body(): lax.all_to_all(expert_out.reshape(sources, MOST, width), 'dp', split_axis...  6.78 us
    all_to_all x1, starting transfers between devices, body(): lax.all_to_all(send_rows, 'dp', split_axis=0, concat_axis=0, tiled=True)  4.37 us
    all_to_all x1, starting transfers between devices, body(): lax.all_to_all(shares.T.astype(jnp.bfloat16), 'dp', split_axis=0, concat_...  3.9 us
    all_to_all x1, starting transfers between devices, body(): lax.all_to_all(expert_out.reshape(sources, MOST, width), 'dp', split_axis...  3.41 us
    dot_general x1, matrix products, feed_forward(): jnp.dot(hidden, down_w, preferred_element_type=jnp.float32)  3.19 us
    dot_general x1, matrix products, feed_forward(): gate_act = jnp.dot(buffer_rows, gate_w, preferred_element_type=jnp.float32)  3.18 us
  transfers between devices with their start and end apart: 4, of which 4 were waited for; matrix products, arithmetic and copies ran while one was open for 19% of the time, Pallas kernels for 0%

commit v1 on v0

v1 whole, which is shorter than its diff:
```python
import jax
import jax.numpy as jnp
from jax import lax
from jax.experimental import pallas as pl
from jax.experimental.pallas import tpu as pltpu
from jax.sharding import PartitionSpec as P

MOST = 6
SLOTS = 8
PARTS = 4
THIRDS = MOST // 2
LONG = 10_000_000_000
VMEM = pl.BlockSpec(memory_space=pltpu.VMEM)
PARAMS = pltpu.CompilerParams(vmem_limit_bytes=16 * 1024 * 1024)


def prep_kernel(picks_ref, out_ref):
    out_ref[...] = picks_ref[...]


def prep(picks):
    return pl.pallas_call(
        prep_kernel,
        out_shape=jax.ShapeDtypeStruct(picks.shape, picks.dtype),
        in_specs=[VMEM],
        out_specs=VMEM,
        compiler_params=PARAMS,
        cost_estimate=pl.CostEstimate(flops=LONG, bytes_accessed=0, transcendentals=0),
        name="prep",
    )(picks)


def select_kernel(ids, table_ref, tokens_ref, send_ref, hot_ref, sorted_ref):
    tok_dev, width = tokens_ref.shape
    n, slots, capacity = sorted_ref.shape
    part = width // PARTS
    me = lax.axis_index("dp").astype(jnp.int32)
    for r, i in enumerate(ids):
        sorted_ref[me ^ i] = jnp.broadcast_to(table_ref[r : r + 1, :], (slots, capacity))
    local = sorted_ref[...] - me * tok_dev
    row = lax.broadcasted_iota(jnp.int32, local.shape, 1)
    lane = lax.broadcasted_iota(jnp.int32, local.shape, 2)
    column = lax.broadcasted_iota(jnp.int32, (n, slots, tok_dev), 2)
    start = jnp.sum((local < 0).astype(jnp.int32), axis=2, keepdims=True)
    place = lane - start
    value = jnp.where((local >= 0) & (local < tok_dev), local + 1, 0)
    hots = []
    for q in range(PARTS):
        if q == 0:
            wanted = jnp.where(row < MOST, row, -1)
        else:
            first, second = q - 1, q - 1 + THIRDS
            wanted = jnp.where(row == MOST, first, jnp.where(row == MOST + 1, second, -1))
        index = jnp.sum(jnp.where(place == wanted, value, 0), axis=2, keepdims=True) - 1
        hot = (index == column).astype(jnp.float32).reshape(n * slots, tok_dev)
        hots.append(hot.astype(jnp.bfloat16))
        hot_ref[q] = hots[q]
    tail = tokens_ref[:, (PARTS - 1) * part :]
    for q in range(PARTS - 1):
        chosen = jnp.dot(
            hots[0], tokens_ref[:, q * part : (q + 1) * part], preferred_element_type=jnp.float32
        ) + jnp.dot(hots[q + 1], tail, preferred_element_type=jnp.float32)
        send_ref[:, :, q * part : (q + 1) * part] = chosen.reshape(n, slots, part).astype(
            jnp.bfloat16
        )


def select(ids, table, tokens):
    tok_dev, width = tokens.shape
    n, capacity = table.shape
    return pl.pallas_call(
        lambda *refs: select_kernel(ids, *refs),
        out_shape=[
            jax.ShapeDtypeStruct((n, SLOTS, width // PARTS * (PARTS - 1)), jnp.bfloat16),
            jax.ShapeDtypeStruct((PARTS, n * SLOTS, tok_dev), jnp.bfloat16),
        ],
        in_specs=[VMEM, VMEM],
        out_specs=[VMEM, VMEM],
        scratch_shapes=[pltpu.VMEM((n, SLOTS, capacity), jnp.int32)],
        compiler_params=PARAMS,
        name="select",
    )(table, tokens)


def ffn_kernel(router_ref, gate_ref, up_ref, down_ref, x_ref, y_ref):
    n, slots, packed = x_ref.shape
    part = packed // (PARTS - 1)
    width = part * PARTS
    rows = n * slots
    experts = router_ref.shape[0]
    me = lax.axis_index("dp").astype(jnp.int32)
    head = x_ref[...].astype(jnp.float32)
    row = lax.broadcasted_iota(jnp.int32, (n, slots, part), 1)
    tail = jnp.zeros((n, slots, part), jnp.float32)
    for q in range(PARTS - 1):
        piece = head[:, :, q * part : (q + 1) * part]
        tail = jnp.where(row == q, piece[:, MOST : MOST + 1], tail)
        tail = jnp.where(row == q + THIRDS, piece[:, MOST + 1 : MOST + 2], tail)
    x = jnp.concatenate([head.reshape(rows, packed), tail.reshape(rows, part)], axis=1)
    x = x.astype(jnp.bfloat16)
    logits = lax.dot_general(
        x, router_ref[...], (((1,), (1,)), ((), ())), preferred_element_type=jnp.float32
    )
    expert_of = lax.broadcasted_iota(jnp.int32, logits.shape, 1)
    top = jnp.max(logits, axis=1, keepdims=True)
    weight = jnp.exp(logits - top)
    total = jnp.sum(weight, axis=1, keepdims=True)
    own = jnp.sum(jnp.where(expert_of == me, weight, 0.0), axis=1, keepdims=True)
    gate_value = (experts * (own / total)).astype(jnp.bfloat16).astype(jnp.float32)
    gate_act = jnp.dot(x, gate_ref[...], preferred_element_type=jnp.float32)
    up_act = jnp.dot(x, up_ref[...], preferred_element_type=jnp.float32)
    silu = gate_act / (1.0 + jnp.exp(-gate_act))
    hidden = (gate_value * silu * up_act).astype(jnp.bfloat16)
    y = jnp.dot(hidden, down_ref[...], preferred_element_type=jnp.float32)
    y = y.reshape(n, slots, width)
    last = y[:, :, packed:]
    for q in range(PARTS - 1):
        piece = y[:, :, q * part : (q + 1) * part]
        piece = jnp.where(row == MOST, last[:, q : q + 1], piece)
        piece = jnp.where(row == MOST + 1, last[:, q + THIRDS : q + THIRDS + 1], piece)
        y_ref[:, :, q * part : (q + 1) * part] = piece.astype(jnp.bfloat16)


def ffn(router_t, w_gate, w_up, w_down, x):
    return pl.pallas_call(
        ffn_kernel,
        out_shape=jax.ShapeDtypeStruct(x.shape, jnp.bfloat16),
        in_specs=[VMEM] * 5,
        out_specs=VMEM,
        compiler_params=PARAMS,
        name="ffn",
    )(router_t, w_gate, w_up, w_down, x)


def spread(hot, rows):
    return lax.dot_general(hot, rows, (((0,), (0,)), ((), ())), preferred_element_type=jnp.float32)


def combine_kernel(hot_ref, y_ref, out_ref, block_ref, sem):
    n, slots, packed = y_ref.shape
    part = packed // (PARTS - 1)
    rows = n * slots
    copies = []
    pieces = [y_ref[:, :, q * part : (q + 1) * part] for q in range(PARTS - 1)]
    pieces = [p.astype(jnp.float32).reshape(rows, part).astype(jnp.bfloat16) for p in pieces]
    for q in range(PARTS):
        if q < PARTS - 1:
            total = spread(hot_ref[0], pieces[q])
        else:
            total = sum(spread(hot_ref[k + 1], pieces[k]) for k in range(PARTS - 1))
        block_ref[q] = total.astype(jnp.bfloat16)
        copy = pltpu.make_async_copy(
            block_ref.at[q], out_ref.at[:, pl.ds(q * part, part)], sem.at[q]
        )
        copy.start()
        copies.append(copy)
    for copy in copies:
        copy.wait()


def combine(hots, y):
    tok_dev = hots.shape[2]
    part = y.shape[2] // (PARTS - 1)
    return pl.pallas_call(
        combine_kernel,
        out_shape=jax.ShapeDtypeStruct((tok_dev, part * PARTS), jnp.bfloat16),
        in_specs=[VMEM, VMEM],
        out_specs=pl.BlockSpec(memory_space=pl.ANY),
        scratch_shapes=[
            pltpu.VMEM((PARTS, tok_dev, part), jnp.bfloat16),
            pltpu.SemaphoreType.DMA((PARTS,)),
        ],
        compiler_params=PARAMS,
        name="combine",
    )(hots, y)


def exchange(value):
    return lax.all_to_all(value, "dp", split_axis=0, concat_axis=0, tiled=True)


def body(tokens, router, w_gate, w_up, w_down, picks):
    n = lax.axis_size("dp")
    known, ids, flip = prep(picks), [0], n // 2
    sent = picks
    while flip:
        got = lax.ppermute(sent, "dp", [(i, i ^ flip) for i in range(n)])
        known = sent = jnp.concatenate([known, got], axis=0)
        ids = ids + [i ^ flip for i in ids]
        flip //= 2
    send, hots = select(ids, known, tokens)
    received = exchange(send)
    y = ffn(router.T, w_gate[0], w_up[0], w_down[0], received)
    return combine(hots, exchange(y))


def solution(mesh):
    return jax.shard_map(
        body,
        mesh=mesh,
        in_specs=(
            P(("rep", "dp"), None),
            P("rep", None),
            P("dp", None, None),
            P("dp", None, None),
            P("dp", None, None),
            P(("rep", "dp"), None),
        ),
        out_specs=P(("rep", "dp"), None),
        check_vma=False,
    )
```

time: 63.7 us -> 40.9 us (0.64)
  blocking collectives: 0 us -> 23.9 us
  waiting for transfers between devices: 17.3 us -> 4.4 us
  starting transfers between devices: 19 us -> 7.92 us
  local copies, waits for them, and re-layouts: 11.3 us -> 0.71 us
  matrix products: 10.3 us -> 0 us
  other arithmetic: 5.13 us -> 0.03 us
  Pallas kernels: 0 us -> 3.69 us
    all_to_all x0 -> x2, blocking collectives: none -> 23.9 us  [exchange(): return lax.all_to_all(value, 'dp', split_axis=0, concat_axis=0, tiled=True)]
    all_to_all x4 -> x0, starting transfers between devices: 19 us -> none  [the longest x1 7.29 us: body(): lax.all_to_all(to_owner, 'dp', split_axis=0, concat_axis=0, tiled=True)]
    all_to_all x4 -> x0, waiting for transfers between devices: 17.3 us -> none  [the longest x1 6.8 us: body(): lax.all_to_all(send_rows, 'dp', split_axis=0, concat_axis=0, tiled=True)]
    dot_general x4 -> x0, matrix products: 10.3 us -> none  [the longest x1 3.19 us: feed_forward(): jnp.dot(hidden, down_w, preferred_element_type=jnp.float32)]
    ppermute x0 -> x3, starting transfers between devices: none -> 7.92 us  [body(): got = lax.ppermute(sent, 'dp', [(i, i ^ flip) for i in range(n)])]
    gather x6 -> x0, local copies, waits for them, and re-layouts: 5.92 us -> none  [the longest x2 3.01 us: body(): tokens[safe_index]]
    ppermute x0 -> x3, waiting for transfers between devices: none -> 4.4 us  [body(): got = lax.ppermute(sent, 'dp', [(i, i ^ flip) for i in range(n)])]
    pallas_call x0 -> x4, Pallas kernels: none -> 3.69 us  [the longest x1 1.81 us: ffn(): pl.pallas_call(ffn_kernel, out_shape=jax.ShapeDtypeStruct(x.shape, jnp.bf...]
  transfers between devices with their start and end apart: 4 -> 3, of which waited for: 4 -> 3; matrix products, arithmetic and copies ran while one was open for 19% -> 0% of each run, Pallas kernels for 0% -> 0%
where the time goes in v1:
time: 40.9 us; the launch traced here: 40.7 us
  blocking collectives  23.9 us (58%)
  starting transfers between devices  7.92 us (19%)
  waiting for transfers between devices  4.4 us (11%)
  Pallas kernels  3.69 us (9%)
  local copies, waits for them, and re-layouts  0.71 us (2%)
    all_to_all x2, blocking collectives, exchange(): return lax.all_to_all(value, 'dp', split_axis=0, concat_axis=0, tiled=True)  23.9 us
    ppermute x3, starting transfers between devices, body(): got = lax.ppermute(sent, 'dp', [(i, i ^ flip) for i in range(n)])  7.92 us
    ppermute x3, waiting for transfers between devices, body(): got = lax.ppermute(sent, 'dp', [(i, i ^ flip) for i in range(n)])  4.4 us
    pallas_call x1, Pallas kernels, ffn(): pl.pallas_call(ffn_kernel, out_shape=jax.ShapeDtypeStruct(x.shape, jnp.bf...  1.81 us
    pallas_call x1, Pallas kernels, combine(): pl.pallas_call(combine_kernel, out_shape=jax.ShapeDtypeStruct((tok_dev, p...  1.34 us
  transfers between devices with their start and end apart: 3, of which 3 were waited for; matrix products, arithmetic and copies ran while one was open for 0% of the time, Pallas kernels for 0%

profile of v1, /device:TPU:0, one launch (start us, length us, event | category | flops | bytes accessed | tf_op | source)
XLA Modules:
  0.0 40.7 jit_solution(17545930796473262679)
XLA Ops:
  0.0 0.0 copy-start.3
  0.0 0.0 copy-start.4
  0.0 4.1 %collective-permute-start = (s32[1,32]{1,0:T(1,128)}, s32[1,32]{1,0:T(1,128)S(1)}, u32[]{:S(2)}, u32[]{:S(2)}) collective-permute-start(s32[1,32]{1,0:T(1,128)} %picks_ref.1), channel_id=1, source_target_pairs={{0,16},{4,20},{8,24},{12,28},{16,0},{20,4},{24,8},{28,12},{1,17},{... | collective-permute-start | bytes 392 | tf_op jit(solution)/shard_map/ppermute | solution.py:187
  4.1 0.0 copy-start.5
  4.1 0.7 %copy-done.5 = s32[1,32]{1,0:T(1,128)S(1)} copy-done((s32[1,32]{1,0:T(1,128)S(1)}, s32[1,32]{1,0:T(1,128)}, u32[]{:S(2)}) %copy-start.5) | copy-done | bytes 152
  4.8 0.0 copy-start
  4.8 0.0 copy-start.1
  4.8 0.0 copy-start.2
  4.8 1.0 %collective-permute-done = s32[1,32]{1,0:T(1,128)S(1)} collective-permute-done((s32[1,32]{1,0:T(1,128)}, s32[1,32]{1,0:T(1,128)S(1)}, u32[]{:S(2)}, u32[]{:S(2)}) %collective-permute-start) | collective-permute-done | bytes 160 | tf_op jit(solution)/shard_map/ppermute | solution.py:187
  5.8 2.0 %collective-permute-start.1 = (s32[2,32]{1,0:T(2,128)S(1)}, s32[2,32]{1,0:T(2,128)S(1)}, u32[]{:S(2)}, u32[]{:S(2)}) collective-permute-start(s32[2,32]{1,0:T(2,128)S(1)} %pad_add_fusion.2), channel_id=1, source_target_pairs={{0,8},{4,12},{8,0},{12,4},{16,24},{20,28},{24,16},{28,20},{1,9},{5... | collective-permute-start | bytes 776 | tf_op jit(solution)/shard_map/ppermute | solution.py:187
  7.7 1.7 %collective-permute-done.1 = s32[2,32]{1,0:T(2,128)S(1)} collective-permute-done((s32[2,32]{1,0:T(2,128)S(1)}, s32[2,32]{1,0:T(2,128)S(1)}, u32[]{:S(2)}, u32[]{:S(2)}) %collective-permute-start.1) | collective-permute-done | bytes 288 | tf_op jit(solution)/shard_map/ppermute | solution.py:187
  9.4 1.9 %collective-permute-start.2 = (s32[4,32]{1,0:T(4,128)S(1)}, s32[4,32]{1,0:T(4,128)S(1)}, u32[]{:S(2)}, u32[]{:S(2)}) collective-permute-start(s32[4,32]{1,0:T(4,128)S(1)} %pad_add_fusion.1), channel_id=1, source_target_pairs={{0,4},{4,0},{8,12},{12,8},{16,20},{20,16},{24,28},{28,24},{1,5},{5... | collective-permute-start | bytes 1544 | tf_op jit(solution)/shard_map/ppermute | solution.py:187
  11.3 1.8 %collective-permute-done.2 = s32[4,32]{1,0:T(4,128)S(1)} collective-permute-done((s32[4,32]{1,0:T(4,128)S(1)}, s32[4,32]{1,0:T(4,128)S(1)}, u32[]{:S(2)}, u32[]{:S(2)}) %collective-permute-start.2) | collective-permute-done | bytes 544 | tf_op jit(solution)/shard_map/ppermute | solution.py:187
  13.1 0.0 copy-done.3
  13.1 0.5 %select.1 = (bf16[8,8,1536]{2,1,0:T(8,128)(2,1)S(1)}, bf16[4,64,256]{2,1,0:T(8,128)(2,1)S(1)}) custom-call(s32[8,32]{1,0:T(8,128)S(1)} %pad_add_fusion.refs_0_, bf16[256,2048]{1,0:T(8,128)(2,1)S(1)} %copy-done.3), custom_call_target="tpu_custom_call" | custom-call | tf_op jit(solution)/shard_map/select/pallas_call | solution.py:71
  13.6 13.7 %all_to_all.10.x_ref = bf16[8,8,1536]{2,1,0:T(8,128)(2,1)S(1)} all-to-all(bf16[8,8,1536]{2,1,0:T(8,128)(2,1)S(1)} %get-tuple-element.8), channel_id=1, replica_groups=mesh['dp'=8,'rep'=4] {'dp'}, dimensions={0} | all-to-all | bytes 393216 | tf_op jit(solution)/shard_map/all_to_all | solution.py:179
  27.3 0.0 copy-done.4
  27.4 0.0 copy-done
  27.4 0.0 copy-done.1
  27.4 0.0 copy-done.2
  27.4 1.8 %ffn.1 = bf16[8,8,1536]{2,1,0:T(8,128)(2,1)S(1)} custom-call(bf16[8,2048]{1,0:T(8,128)(2,1)S(1)} %bitcast.7, bf16[2048,768]{1,0:T(8,128)(2,1)S(1)} %bitcast.4, bf16[2048,768]{1,0:T(8,128)(2,1)S(1)} %bitcast.5, bf16[768,2048]{1,0:T(8,128)(2,1)S(1)} %bitcast.6, bf16[8,8,1536]{2,1,0:T(8,128)(2,1)S(1)} %all_to_all.10.x_ref), custom_call_target="tpu_custom_call" | custom-call | tf_op jit(solution)/shard_map/ffn/pallas_call | solution.py:125
  29.2 10.2 %all_to_all.11.y_ref = bf16[8,8,1536]{2,1,0:T(8,128)(2,1)S(1)} all-to-all(bf16[8,8,1536]{2,1,0:T(8,128)(2,1)S(1)} %ffn.1), channel_id=1, replica_groups=mesh['dp'=8,'rep'=4] {'dp'}, dimensions={0} | all-to-all | bytes 393216 | tf_op jit(solution)/shard_map/all_to_all | solution.py:179
  39.4 1.3 %combine.1 = bf16[256,2048]{1,0:T(8,128)(2,1)} custom-call(bf16[4,64,256]{2,1,0:T(8,128)(2,1)S(1)} %get-tuple-element.7.hot_ref, bf16[8,8,1536]{2,1,0:T(8,128)(2,1)S(1)} %all_to_all.11.y_ref), custom_call_target="tpu_custom_call" | custom-call | tf_op jit(solution)/shard_map/combine/pallas_call | solution.py:164
  (4 shorter events, 0.0 us)
Async XLA Ops:
  0.0 13.1 %copy-start.3 = (bf16[256,2048]{1,0:T(8,128)(2,1)S(1)}, bf16[256,2048]{1,0:T(8,128)(2,1)}, u32[]{:S(2)}) copy-start(bf16[256,2048]{1,0:T(8,128)(2,1)} %refs_1_.1) | copy-start | bytes 3145732
  0.0 27.3 %copy-start.4 = (bf16[2048,8]{0,1:T(8,128)(2,1)S(1)}, bf16[2048,8]{0,1:T(8,128)(2,1)}, u32[]{:S(2)}) copy-start(bf16[2048,8]{0,1:T(8,128)(2,1)} %param.7) | copy-start | bytes 98308
  0.0 5.7 %collective-permute-start = (s32[1,32]{1,0:T(1,128)}, s32[1,32]{1,0:T(1,128)S(1)}, u32[]{:S(2)}, u32[]{:S(2)}) collective-permute-start(s32[1,32]{1,0:T(1,128)} %picks_ref.1), channel_id=1, source_target_pairs={{0,16},{4,20},{8,24},{12,28},{16,0},{20,4},{24,8},{28,12},{1,17},{... | collective-permute-start | bytes 392 | tf_op jit(solution)/shard_map/ppermute | solution.py:187
  4.1 0.7 %copy-start.5 = (s32[1,32]{1,0:T(1,128)S(1)}, s32[1,32]{1,0:T(1,128)}, u32[]{:S(2)}) copy-start(s32[1,32]{1,0:T(1,128)} %picks_ref.1) | copy-start | bytes 388
  4.8 22.6 %copy-start = (bf16[1,2048,768]{2,1,0:T(8,128)(2,1)S(1)}, bf16[1,2048,768]{2,1,0:T(8,128)(2,1)}, u32[]{:S(2)}) copy-start(bf16[1,2048,768]{2,1,0:T(8,128)(2,1)} %param.8) | copy-start | bytes 9437188
  4.8 22.6 %copy-start.1 = (bf16[1,2048,768]{2,1,0:T(8,128)(2,1)S(1)}, bf16[1,2048,768]{2,1,0:T(8,128)(2,1)}, u32[]{:S(2)}) copy-start(bf16[1,2048,768]{2,1,0:T(8,128)(2,1)} %param.9) | copy-start | bytes 9437188
  4.8 22.6 %copy-start.2 = (bf16[1,768,2048]{2,1,0:T(8,128)(2,1)S(1)}, bf16[1,768,2048]{2,1,0:T(8,128)(2,1)}, u32[]{:S(2)}) copy-start(bf16[1,768,2048]{2,1,0:T(8,128)(2,1)} %param.10) | copy-start | bytes 9437188
  5.8 3.6 %collective-permute-start.1 = (s32[2,32]{1,0:T(2,128)S(1)}, s32[2,32]{1,0:T(2,128)S(1)}, u32[]{:S(2)}, u32[]{:S(2)}) collective-permute-start(s32[2,32]{1,0:T(2,128)S(1)} %pad_add_fusion.2), channel_id=1, source_target_pairs={{0,8},{4,12},{8,0},{12,4},{16,24},{20,28},{24,16},{28,20},{1,9},{5... | collective-permute-start | bytes 776 | tf_op jit(solution)/shard_map/ppermute | solution.py:187
  9.4 3.7 %collective-permute-start.2 = (s32[4,32]{1,0:T(4,128)S(1)}, s32[4,32]{1,0:T(4,128)S(1)}, u32[]{:S(2)}, u32[]{:S(2)}) collective-permute-start(s32[4,32]{1,0:T(4,128)S(1)} %pad_add_fusion.1), channel_id=1, source_target_pairs={{0,4},{4,0},{8,12},{12,8},{16,20},{20,16},{24,28},{28,24},{1,5},{5... | collective-permute-start | bytes 1544 | tf_op jit(solution)/shard_map/ppermute | solution.py:187

commit v2 on v1

--- a/solution.py
+++ b/solution.py
@@ -14,30 +14,30 @@
 PARAMS = pltpu.CompilerParams(vmem_limit_bytes=16 * 1024 * 1024)
 
 
-def prep_kernel(picks_ref, out_ref):
-    out_ref[...] = picks_ref[...]
-
-
-def prep(picks):
-    return pl.pallas_call(
-        prep_kernel,
-        out_shape=jax.ShapeDtypeStruct(picks.shape, picks.dtype),
+def spread_kernel(picks_ref, out_ref):
+    out_ref[...] = jnp.broadcast_to(picks_ref[...][None], out_ref.shape)
+
+
+def spread(picks, n):
+    return pl.pallas_call(
+        spread_kernel,
+        out_shape=jax.ShapeDtypeStruct((n,) + picks.shape, picks.dtype),
         in_specs=[VMEM],
         out_specs=VMEM,
         compiler_params=PARAMS,
         cost_estimate=pl.CostEstimate(flops=LONG, bytes_accessed=0, transcendentals=0),
-        name="prep",
+        name="spread",
     )(picks)
 
 
-def select_kernel(ids, table_ref, tokens_ref, send_ref, hot_ref, sorted_ref):
+def select_kernel(table_ref, tokens_ref, send_ref, hot_ref):
     tok_dev, width = tokens_ref.shape
-    n, slots, capacity = sorted_ref.shape
+    n, slots, _ = send_ref.shape
+    capacity = table_ref.shape[2]
     part = width // PARTS
     me = lax.axis_index("dp").astype(jnp.int32)
-    for r, i in enumerate(ids):
-        sorted_ref[me ^ i] = jnp.broadcast_to(table_ref[r : r + 1, :], (slots, capacity))
-    local = sorted_ref[...] - me * tok_dev
+    table = jnp.broadcast_to(table_ref[...], (n, slots, capacity))
+    local = table - me * tok_dev
     row = lax.broadcasted_iota(jnp.int32, local.shape, 1)
     lane = lax.broadcasted_iota(jnp.int32, local.shape, 2)
     column = lax.broadcasted_iota(jnp.int32, (n, slots, tok_dev), 2)
@@ -65,18 +65,17 @@
         )
 
 
-def select(ids, table, tokens):
+def select(table, tokens):
     tok_dev, width = tokens.shape
-    n, capacity = table.shape
-    return pl.pallas_call(
-        lambda *refs: select_kernel(ids, *refs),
+    n = table.shape[0]
+    return pl.pallas_call(
+        select_kernel,
         out_shape=[
             jax.ShapeDtypeStruct((n, SLOTS, width // PARTS * (PARTS - 1)), jnp.bfloat16),
             jax.ShapeDtypeStruct((PARTS, n * SLOTS, tok_dev), jnp.bfloat16),
         ],
         in_specs=[VMEM, VMEM],
         out_specs=[VMEM, VMEM],
-        scratch_shapes=[pltpu.VMEM((n, SLOTS, capacity), jnp.int32)],
         compiler_params=PARAMS,
         name="select",
     )(table, tokens)
@@ -132,7 +131,7 @@
     )(router_t, w_gate, w_up, w_down, x)
 
 
-def spread(hot, rows):
+def place(hot, rows):
     return lax.dot_general(hot, rows, (((0,), (0,)), ((), ())), preferred_element_type=jnp.float32)
 
 
@@ -145,9 +144,9 @@
     pieces = [p.astype(jnp.float32).reshape(rows, part).astype(jnp.bfloat16) for p in pieces]
     for q in range(PARTS):
         if q < PARTS - 1:
-            total = spread(hot_ref[0], pieces[q])
+            total = place(hot_ref[0], pieces[q])
         else:
-            total = sum(spread(hot_ref[k + 1], pieces[k]) for k in range(PARTS - 1))
+            total = sum(place(hot_ref[k + 1], pieces[k]) for k in range(PARTS - 1))
         block_ref[q] = total.astype(jnp.bfloat16)
         copy = pltpu.make_async_copy(
             block_ref.at[q], out_ref.at[:, pl.ds(q * part, part)], sem.at[q]
@@ -176,19 +175,16 @@
 
 
 def exchange(value):
-    return lax.all_to_all(value, "dp", split_axis=0, concat_axis=0, tiled=True)
+    n = lax.axis_size("dp")
+    order = [(n // 2 + 1 - k) % n for k in range(n)]
+    return lax.all_to_all(
+        value, "dp", split_axis=0, concat_axis=0, tiled=True, axis_index_groups=[order]
+    )
 
 
 def body(tokens, router, w_gate, w_up, w_down, picks):
     n = lax.axis_size("dp")
-    known, ids, flip = prep(picks), [0], n // 2
-    sent = picks
-    while flip:
-        got = lax.ppermute(sent, "dp", [(i, i ^ flip) for i in range(n)])
-        known = sent = jnp.concatenate([known, got], axis=0)
-        ids = ids + [i ^ flip for i in ids]
-        flip //= 2
-    send, hots = select(ids, known, tokens)
+    send, hots = select(exchange(spread(picks, n)), tokens)
     received = exchange(send)
     y = ffn(router.T, w_gate[0], w_up[0], w_down[0], received)
     return combine(hots, exchange(y))

time: 40.9 us -> 34.1 us (0.83)
  starting transfers between devices: 7.92 us -> 0 us
  blocking collectives: 23.9 us -> 29.3 us
  waiting for transfers between devices: 4.4 us -> 0 us
    ppermute x3 -> x0, starting transfers between devices: 7.92 us -> none  [body(): got = lax.ppermute(sent, 'dp', [(i, i ^ flip) for i in range(n)])]
    all_to_all x2 -> x3, blocking collectives: 23.9 us -> 29.3 us  [exchange(): lax.all_to_all(value, 'dp', split_axis=0, concat_axis=0, tiled=True, axis...]
    ppermute x3 -> x0, waiting for transfers between devices: 4.4 us -> none  [body(): got = lax.ppermute(sent, 'dp', [(i, i ^ flip) for i in range(n)])]
  transfers between devices with their start and end apart: 3 -> 0, of which waited for: 3 -> 0; matrix products, arithmetic and copies ran while one was open for 0% -> 0% of each run, Pallas kernels for 0% -> 0%
where the time goes in v2:
time: 34.1 us; the launch traced here: 33.8 us
  blocking collectives  29.3 us (86%)
  Pallas kernels  3.67 us (11%)
  local copies, waits for them, and re-layouts  0.76 us (2%)
    all_to_all x3, blocking collectives, exchange(): lax.all_to_all(value, 'dp', split_axis=0, concat_axis=0, tiled=True, axis...  29.3 us
    pallas_call x1, Pallas kernels, ffn(): pl.pallas_call(ffn_kernel, out_shape=jax.ShapeDtypeStruct(x.shape, jnp.bf...  1.81 us
    pallas_call x1, Pallas kernels, combine(): pl.pallas_call(combine_kernel, out_shape=jax.ShapeDtypeStruct((tok_dev, p...  1.33 us
    unnamed x12, local copies, waits for them, and re-layouts  0.76 us

profile of v2, /device:TPU:0, one launch (start us, length us, event | category | flops | bytes accessed | tf_op | source)
XLA Modules:
  0.0 33.8 jit_solution(9135136627830408287)
XLA Ops:
  0.0 0.0 copy-start.3
  0.0 0.0 copy-start.5
  0.0 0.7 %copy-done.5 = s32[1,32]{1,0:T(1,128)S(1)} copy-done((s32[1,32]{1,0:T(1,128)S(1)}, s32[1,32]{1,0:T(1,128)}, u32[]{:S(2)}) %copy-start.5) | copy-done | bytes 152
  0.7 0.0 copy-start
  0.7 0.0 copy-start.1
  0.8 0.0 copy-start.2
  0.8 0.0 copy-start.4
  0.8 11.1 %all_to_all.15.table_ref = s32[8,1,32]{2,1,0:T(1,128)S(1)} all-to-all(s32[8,1,32]{2,1,0:T(1,128)S(1)} %spread.1), channel_id=1, replica_groups={{20,16,12,8,4,0,28,24},{21,17,13,9,5,1,29,25},{22,18,14,10,6,2,30,26},{..., dimensions={0} | all-to-all | bytes 2048 | tf_op jit(solution)/shard_map/all_to_all | solution.py:180
  11.9 0.0 copy-done.3
  11.9 0.5 %select.1 = (bf16[8,8,1536]{2,1,0:T(8,128)(2,1)S(1)}, bf16[4,64,256]{2,1,0:T(8,128)(2,1)S(1)}) custom-call(s32[8,1,32]{2,1,0:T(1,128)S(1)} %all_to_all.15.table_ref, bf16[256,2048]{1,0:T(8,128)(2,1)S(1)} %copy-done.3), custom_call_target="tpu_custom_call" | custom-call | tf_op jit(solution)/shard_map/select/pallas_call | solution.py:71
  12.4 8.8 %all_to_all.16.x_ref = bf16[8,8,1536]{2,1,0:T(8,128)(2,1)S(1)} all-to-all(bf16[8,8,1536]{2,1,0:T(8,128)(2,1)S(1)} %get-tuple-element.8), channel_id=1, replica_groups={{20,16,12,8,4,0,28,24},{21,17,13,9,5,1,29,25},{22,18,14,10,6,2,30,26},{..., dimensions={0} | all-to-all | bytes 393216 | tf_op jit(solution)/shard_map/all_to_all | solution.py:180
  21.2 0.0 copy-done
  21.2 0.0 copy-done.1
  21.2 0.0 copy-done.2
  21.3 0.0 copy-done.4
  21.3 1.8 %ffn.1 = bf16[8,8,1536]{2,1,0:T(8,128)(2,1)S(1)} custom-call(bf16[8,2048]{1,0:T(8,128)(2,1)S(1)} %bitcast.7, bf16[2048,768]{1,0:T(8,128)(2,1)S(1)} %bitcast.4, bf16[2048,768]{1,0:T(8,128)(2,1)S(1)} %bitcast.5, bf16[768,2048]{1,0:T(8,128)(2,1)S(1)} %bitcast.6, bf16[8,8,1536]{2,1,0:T(8,128)(2,1)S(1)} %all_to_all.16.x_ref), custom_call_target="tpu_custom_call" | custom-call | tf_op jit(solution)/shard_map/ffn/pallas_call | solution.py:124
  23.1 9.4 %all_to_all.17.y_ref = bf16[8,8,1536]{2,1,0:T(8,128)(2,1)S(1)} all-to-all(bf16[8,8,1536]{2,1,0:T(8,128)(2,1)S(1)} %ffn.1), channel_id=1, replica_groups={{20,16,12,8,4,0,28,24},{21,17,13,9,5,1,29,25},{22,18,14,10,6,2,30,26},{..., dimensions={0} | all-to-all | bytes 393216 | tf_op jit(solution)/shard_map/all_to_all | solution.py:180
  32.5 1.3 %combine.1 = bf16[256,2048]{1,0:T(8,128)(2,1)} custom-call(bf16[4,64,256]{2,1,0:T(8,128)(2,1)S(1)} %get-tuple-element.7.hot_ref, bf16[8,8,1536]{2,1,0:T(8,128)(2,1)S(1)} %all_to_all.17.y_ref), custom_call_target="tpu_custom_call" | custom-call | tf_op jit(solution)/shard_map/combine/pallas_call | solution.py:163
  (1 shorter events, 0.0 us)
Async XLA Ops:
  0.0 11.9 %copy-start.3 = (bf16[256,2048]{1,0:T(8,128)(2,1)S(1)}, bf16[256,2048]{1,0:T(8,128)(2,1)}, u32[]{:S(2)}) copy-start(bf16[256,2048]{1,0:T(8,128)(2,1)} %tokens_ref.1) | copy-start | bytes 3145732
  0.0 0.7 %copy-start.5 = (s32[1,32]{1,0:T(1,128)S(1)}, s32[1,32]{1,0:T(1,128)}, u32[]{:S(2)}) copy-start(s32[1,32]{1,0:T(1,128)} %picks_ref.1) | copy-start | bytes 388
  0.7 20.5 %copy-start = (bf16[1,2048,768]{2,1,0:T(8,128)(2,1)S(1)}, bf16[1,2048,768]{2,1,0:T(8,128)(2,1)}, u32[]{:S(2)}) copy-start(bf16[1,2048,768]{2,1,0:T(8,128)(2,1)} %param.8) | copy-start | bytes 9437188
  0.7 20.5 %copy-start.1 = (bf16[1,2048,768]{2,1,0:T(8,128)(2,1)S(1)}, bf16[1,2048,768]{2,1,0:T(8,128)(2,1)}, u32[]{:S(2)}) copy-start(bf16[1,2048,768]{2,1,0:T(8,128)(2,1)} %param.9) | copy-start | bytes 9437188
  0.8 20.5 %copy-start.2 = (bf16[1,768,2048]{2,1,0:T(8,128)(2,1)S(1)}, bf16[1,768,2048]{2,1,0:T(8,128)(2,1)}, u32[]{:S(2)}) copy-start(bf16[1,768,2048]{2,1,0:T(8,128)(2,1)} %param.10) | copy-start | bytes 9437188
  0.8 20.5 %copy-start.4 = (bf16[2048,8]{0,1:T(8,128)(2,1)S(1)}, bf16[2048,8]{0,1:T(8,128)(2,1)}, u32[]{:S(2)}) copy-start(bf16[2048,8]{0,1:T(8,128)(2,1)} %param.7) | copy-start | bytes 98308

commit v3 on v2

--- a/solution.py
+++ b/solution.py
@@ -14,20 +14,20 @@
 PARAMS = pltpu.CompilerParams(vmem_limit_bytes=16 * 1024 * 1024)
 
 
-def spread_kernel(picks_ref, out_ref):
-    out_ref[...] = jnp.broadcast_to(picks_ref[...][None], out_ref.shape)
-
-
-def spread(picks, n):
-    return pl.pallas_call(
-        spread_kernel,
-        out_shape=jax.ShapeDtypeStruct((n,) + picks.shape, picks.dtype),
+def hold_kernel(in_ref, out_ref):
+    out_ref[...] = in_ref[...]
+
+
+def hold(value):
+    return pl.pallas_call(
+        hold_kernel,
+        out_shape=jax.ShapeDtypeStruct(value.shape, value.dtype),
         in_specs=[VMEM],
         out_specs=VMEM,
         compiler_params=PARAMS,
         cost_estimate=pl.CostEstimate(flops=LONG, bytes_accessed=0, transcendentals=0),
-        name="spread",
-    )(picks)
+        name="hold",
+    )(value)
 
 
 def select_kernel(table_ref, tokens_ref, send_ref, hot_ref):
@@ -54,7 +54,7 @@
         index = jnp.sum(jnp.where(place == wanted, value, 0), axis=2, keepdims=True) - 1
         hot = (index == column).astype(jnp.float32).reshape(n * slots, tok_dev)
         hots.append(hot.astype(jnp.bfloat16))
-        hot_ref[q] = hots[q]
+        hot_ref[q * n * slots : (q + 1) * n * slots] = hots[q]
     tail = tokens_ref[:, (PARTS - 1) * part :]
     for q in range(PARTS - 1):
         chosen = jnp.dot(
@@ -72,7 +72,7 @@
         select_kernel,
         out_shape=[
             jax.ShapeDtypeStruct((n, SLOTS, width // PARTS * (PARTS - 1)), jnp.bfloat16),
-            jax.ShapeDtypeStruct((PARTS, n * SLOTS, tok_dev), jnp.bfloat16),
+            jax.ShapeDtypeStruct((PARTS * n * SLOTS, tok_dev), jnp.bfloat16),
         ],
         in_specs=[VMEM, VMEM],
         out_specs=[VMEM, VMEM],
@@ -142,11 +142,12 @@
     copies = []
     pieces = [y_ref[:, :, q * part : (q + 1) * part] for q in range(PARTS - 1)]
     pieces = [p.astype(jnp.float32).reshape(rows, part).astype(jnp.bfloat16) for p in pieces]
+    head = hot_ref[:rows]
     for q in range(PARTS):
         if q < PARTS - 1:
-            total = place(hot_ref[0], pieces[q])
+            total = place(head, pieces[q])
         else:
-            total = sum(place(hot_ref[k + 1], pieces[k]) for k in range(PARTS - 1))
+            total = place(hot_ref[rows:], jnp.concatenate(pieces, axis=0))
         block_ref[q] = total.astype(jnp.bfloat16)
         copy = pltpu.make_async_copy(
             block_ref.at[q], out_ref.at[:, pl.ds(q * part, part)], sem.at[q]
@@ -158,7 +159,7 @@
 
 
 def combine(hots, y):
-    tok_dev = hots.shape[2]
+    tok_dev = hots.shape[1]
     part = y.shape[2] // (PARTS - 1)
     return pl.pallas_call(
         combine_kernel,
@@ -184,7 +185,7 @@
 
 def body(tokens, router, w_gate, w_up, w_down, picks):
     n = lax.axis_size("dp")
-    send, hots = select(exchange(spread(picks, n)), tokens)
+    send, hots = select(exchange(hold(jnp.broadcast_to(picks[None], (n,) + picks.shape))), tokens)
     received = exchange(send)
     y = ffn(router.T, w_gate[0], w_up[0], w_down[0], received)
     return combine(hots, exchange(y))

time: 34.1 us -> 33.9 us (level)
    unnamed x12 -> x10, local copies, waits for them, and re-layouts: 0.76 us -> 0.02 us
    broadcast_in_dim x0 -> x1, local copies, waits for them, and re-layouts: none -> 0.66 us  [body(): jnp.broadcast_to(picks[None], (n,) + picks.shape)]
where the time goes in v3:
time: 33.9 us; the launch traced here: 33.7 us
  blocking collectives  29.3 us (86%)
  Pallas kernels  3.58 us (11%)
  local copies, waits for them, and re-layouts  0.68 us (2%)
    all_to_all x3, blocking collectives, exchange(): lax.all_to_all(value, 'dp', split_axis=0, concat_axis=0, tiled=True, axis...  29.3 us
    pallas_call x1, Pallas kernels, ffn(): pl.pallas_call(ffn_kernel, out_shape=jax.ShapeDtypeStruct(x.shape, jnp.bf...  1.81 us
    pallas_call x1, Pallas kernels, combine(): pl.pallas_call(combine_kernel, out_shape=jax.ShapeDtypeStruct((tok_dev, p...  1.24 us

profile of v3, /device:TPU:0, one launch (start us, length us, event | category | flops | bytes accessed | tf_op | source)
XLA Modules:
  0.0 33.7 jit_solution(2998701526654310372)
XLA Ops:
  0.0 0.7 %broadcast_in_dim.9.in_ref = s32[8,1,32]{2,1,0:T(1,128)S(1)} broadcast(s32[32]{0:T(128)} %bitcast.9), dimensions={2} | broadcast | bytes 1152 | tf_op jit(solution)/shard_map/broadcast_in_dim | solution.py:188
  0.7 0.0 copy-start.3
  0.7 0.0 copy-start
  0.7 0.0 copy-start.1
  0.7 0.0 copy-start.2
  0.7 0.0 copy-start.4
  0.7 11.1 %all_to_all.15.table_ref = s32[8,1,32]{2,1,0:T(1,128)S(1)} all-to-all(s32[8,1,32]{2,1,0:T(1,128)S(1)} %hold.1), channel_id=1, replica_groups={{20,16,12,8,4,0,28,24},{21,17,13,9,5,1,29,25},{22,18,14,10,6,2,30,26},{..., dimensions={0} | all-to-all | bytes 2048 | tf_op jit(solution)/shard_map/all_to_all | solution.py:181
  11.8 0.0 copy-done.3
  11.8 0.5 %select.1 = (bf16[8,8,1536]{2,1,0:T(8,128)(2,1)S(1)}, bf16[256,256]{1,0:T(8,128)(2,1)S(1)}) custom-call(s32[8,1,32]{2,1,0:T(1,128)S(1)} %all_to_all.15.table_ref, bf16[256,2048]{1,0:T(8,128)(2,1)S(1)} %copy-done.3), custom_call_target="tpu_custom_call" | custom-call | tf_op jit(solution)/shard_map/select/pallas_call | solution.py:71
  12.4 8.8 %all_to_all.16.x_ref = bf16[8,8,1536]{2,1,0:T(8,128)(2,1)S(1)} all-to-all(bf16[8,8,1536]{2,1,0:T(8,128)(2,1)S(1)} %get-tuple-element.8), channel_id=1, replica_groups={{20,16,12,8,4,0,28,24},{21,17,13,9,5,1,29,25},{22,18,14,10,6,2,30,26},{..., dimensions={0} | all-to-all | bytes 393216 | tf_op jit(solution)/shard_map/all_to_all | solution.py:181
  21.2 0.0 copy-done
  21.2 0.0 copy-done.1
  21.2 0.0 copy-done.2
  21.2 0.0 copy-done.4
  21.2 1.8 %ffn.1 = bf16[8,8,1536]{2,1,0:T(8,128)(2,1)S(1)} custom-call(bf16[8,2048]{1,0:T(8,128)(2,1)S(1)} %bitcast.8, bf16[2048,768]{1,0:T(8,128)(2,1)S(1)} %bitcast.5, bf16[2048,768]{1,0:T(8,128)(2,1)S(1)} %bitcast.6, bf16[768,2048]{1,0:T(8,128)(2,1)S(1)} %bitcast.7, bf16[8,8,1536]{2,1,0:T(8,128)(2,1)S(1)} %all_to_all.16.x_ref), custom_call_target="tpu_custom_call" | custom-call | tf_op jit(solution)/shard_map/ffn/pallas_call | solution.py:124
  23.0 9.4 %all_to_all.17.y_ref = bf16[8,8,1536]{2,1,0:T(8,128)(2,1)S(1)} all-to-all(bf16[8,8,1536]{2,1,0:T(8,128)(2,1)S(1)} %ffn.1), channel_id=1, replica_groups={{20,16,12,8,4,0,28,24},{21,17,13,9,5,1,29,25},{22,18,14,10,6,2,30,26},{..., dimensions={0} | all-to-all | bytes 393216 | tf_op jit(solution)/shard_map/all_to_all | solution.py:181
  32.4 1.2 %combine.1 = bf16[256,2048]{1,0:T(8,128)(2,1)} custom-call(bf16[256,256]{1,0:T(8,128)(2,1)S(1)} %get-tuple-element.7.hot_ref, bf16[8,8,1536]{2,1,0:T(8,128)(2,1)S(1)} %all_to_all.17.y_ref), custom_call_target="tpu_custom_call" | custom-call | tf_op jit(solution)/shard_map/combine/pallas_call | solution.py:164
  (1 shorter events, 0.0 us)
Async XLA Ops:
  0.7 11.2 %copy-start.3 = (bf16[256,2048]{1,0:T(8,128)(2,1)S(1)}, bf16[256,2048]{1,0:T(8,128)(2,1)}, u32[]{:S(2)}) copy-start(bf16[256,2048]{1,0:T(8,128)(2,1)} %tokens_ref.1) | copy-start | bytes 3145732
  0.7 20.5 %copy-start = (bf16[1,2048,768]{2,1,0:T(8,128)(2,1)S(1)}, bf16[1,2048,768]{2,1,0:T(8,128)(2,1)}, u32[]{:S(2)}) copy-start(bf16[1,2048,768]{2,1,0:T(8,128)(2,1)} %param.8) | copy-start | bytes 9437188
  0.7 20.5 %copy-start.1 = (bf16[1,2048,768]{2,1,0:T(8,128)(2,1)S(1)}, bf16[1,2048,768]{2,1,0:T(8,128)(2,1)}, u32[]{:S(2)}) copy-start(bf16[1,2048,768]{2,1,0:T(8,128)(2,1)} %param.9) | copy-start | bytes 9437188
  0.7 20.5 %copy-start.2 = (bf16[1,768,2048]{2,1,0:T(8,128)(2,1)S(1)}, bf16[1,768,2048]{2,1,0:T(8,128)(2,1)}, u32[]{:S(2)}) copy-start(bf16[1,768,2048]{2,1,0:T(8,128)(2,1)} %param.10) | copy-start | bytes 9437188
  0.7 20.5 %copy-start.4 = (bf16[2048,8]{0,1:T(8,128)(2,1)S(1)}, bf16[2048,8]{0,1:T(8,128)(2,1)}, u32[]{:S(2)}) copy-start(bf16[2048,8]{0,1:T(8,128)(2,1)} %param.7) | copy-start | bytes 98308

commit v4 on v3

--- a/solution.py
+++ b/solution.py
@@ -10,6 +10,7 @@
 PARTS = 4
 THIRDS = MOST // 2
 LONG = 10_000_000_000
+TALL = 128
 VMEM = pl.BlockSpec(memory_space=pltpu.VMEM)
 PARAMS = pltpu.CompilerParams(vmem_limit_bytes=16 * 1024 * 1024)
 
@@ -55,11 +56,17 @@
         hot = (index == column).astype(jnp.float32).reshape(n * slots, tok_dev)
         hots.append(hot.astype(jnp.bfloat16))
         hot_ref[q * n * slots : (q + 1) * n * slots] = hots[q]
-    tail = tokens_ref[:, (PARTS - 1) * part :]
+    rows = n * slots
+    tails = jnp.dot(
+        jnp.concatenate(hots[1:], axis=0),
+        tokens_ref[:, (PARTS - 1) * part :],
+        preferred_element_type=jnp.float32,
+    )
     for q in range(PARTS - 1):
         chosen = jnp.dot(
             hots[0], tokens_ref[:, q * part : (q + 1) * part], preferred_element_type=jnp.float32
-        ) + jnp.dot(hots[q + 1], tail, preferred_element_type=jnp.float32)
+        )
+        chosen = chosen + tails[q * rows : (q + 1) * rows]
         send_ref[:, :, q * part : (q + 1) * part] = chosen.reshape(n, slots, part).astype(
             jnp.bfloat16
         )
@@ -106,11 +113,19 @@
     total = jnp.sum(weight, axis=1, keepdims=True)
     own = jnp.sum(jnp.where(expert_of == me, weight, 0.0), axis=1, keepdims=True)
     gate_value = (experts * (own / total)).astype(jnp.bfloat16).astype(jnp.float32)
-    gate_act = jnp.dot(x, gate_ref[...], preferred_element_type=jnp.float32)
-    up_act = jnp.dot(x, up_ref[...], preferred_element_type=jnp.float32)
+
+    def product(left, right):
+        if 2 * rows > TALL:
+            return jnp.dot(left, right, preferred_element_type=jnp.float32)
+        tall = jnp.concatenate([left, jnp.zeros_like(left)], axis=0)
+        both = jnp.dot(tall, right, preferred_element_type=jnp.float32)
+        return both[:rows] + both[rows:]
+
+    gate_act = product(x, gate_ref[...])
+    up_act = product(x, up_ref[...])
     silu = gate_act / (1.0 + jnp.exp(-gate_act))
     hidden = (gate_value * silu * up_act).astype(jnp.bfloat16)
-    y = jnp.dot(hidden, down_ref[...], preferred_element_type=jnp.float32)
+    y = product(hidden, down_ref[...])
     y = y.reshape(n, slots, width)
     last = y[:, :, packed:]
     for q in range(PARTS - 1):
@@ -175,11 +190,21 @@
     )(hots, y)
 
 
+def ring(n):
+    if n & (n - 1):
+        return [(n // 2 + 1 - k) % n for k in range(n)]
+    codes = [k ^ (k >> 1) for k in range(n)]
+    return [(n // 2 + 1) % n ^ (c >> 1) ^ ((c & 1) * (n // 2)) for c in codes]
+
+
 def exchange(value):
-    n = lax.axis_size("dp")
-    order = [(n // 2 + 1 - k) % n for k in range(n)]
     return lax.all_to_all(
-        value, "dp", split_axis=0, concat_axis=0, tiled=True, axis_index_groups=[order]
+        value,
+        "dp",
+        split_axis=0,
+        concat_axis=0,
+        tiled=True,
+        axis_index_groups=[ring(lax.axis_size("dp"))],
     )
 
 

time: 33.9 us -> 33.3 us (0.982)
  blocking collectives: 29.3 us -> 28.9 us
    all_to_all x3, blocking collectives: 29.3 us -> 28.9 us  [exchange(): lax.all_to_all(value, 'dp', split_axis=0, concat_axis=0, tiled=True, axis...]
where the time goes in v4:
time: 33.3 us; the launch traced here: 33.1 us
  blocking collectives  28.9 us (87%)
  Pallas kernels  3.45 us (10%)
  local copies, waits for them, and re-layouts  0.68 us (2%)
    all_to_all x3, blocking collectives, exchange(): lax.all_to_all(value, 'dp', split_axis=0, concat_axis=0, tiled=True, axis...  28.9 us
    pallas_call x1, Pallas kernels, ffn(): pl.pallas_call(ffn_kernel, out_shape=jax.ShapeDtypeStruct(x.shape, jnp.bf...  1.75 us
    pallas_call x1, Pallas kernels, combine(): pl.pallas_call(combine_kernel, out_shape=jax.ShapeDtypeStruct((tok_dev, p...  1.25 us

profile of v4, /device:TPU:0, one launch (start us, length us, event | category | flops | bytes accessed | tf_op | source)
XLA Modules:
  0.0 33.1 jit_solution(2114661960966787037)
XLA Ops:
  0.0 0.7 %broadcast_in_dim.9.in_ref = s32[8,1,32]{2,1,0:T(1,128)S(1)} broadcast(s32[32]{0:T(128)} %bitcast.9), dimensions={2} | broadcast | bytes 1152 | tf_op jit(solution)/shard_map/broadcast_in_dim | solution.py:213
  0.7 0.0 copy-start.3
  0.7 0.0 copy-start
  0.7 0.0 copy-start.1
  0.7 0.0 copy-start.2
  0.7 0.0 copy-start.4
  0.7 11.1 %all_to_all.15.table_ref = s32[8,1,32]{2,1,0:T(1,128)S(1)} all-to-all(s32[8,1,32]{2,1,0:T(1,128)S(1)} %hold.1), channel_id=1, replica_groups={{20,4,0,16,24,8,12,28},{21,5,1,17,25,9,13,29},{22,6,2,18,26,10,14,30},{..., dimensions={0} | all-to-all | bytes 2048 | tf_op jit(solution)/shard_map/all_to_all | solution.py:201
  11.8 0.0 copy-done.3
  11.8 0.5 %select.1 = (bf16[8,8,1536]{2,1,0:T(8,128)(2,1)S(1)}, bf16[256,256]{1,0:T(8,128)(2,1)S(1)}) custom-call(s32[8,1,32]{2,1,0:T(1,128)S(1)} %all_to_all.15.table_ref, bf16[256,2048]{1,0:T(8,128)(2,1)S(1)} %copy-done.3), custom_call_target="tpu_custom_call" | custom-call | tf_op jit(solution)/shard_map/select/pallas_call | solution.py:78
  12.3 8.6 %all_to_all.16.x_ref = bf16[8,8,1536]{2,1,0:T(8,128)(2,1)S(1)} all-to-all(bf16[8,8,1536]{2,1,0:T(8,128)(2,1)S(1)} %get-tuple-element.8), channel_id=1, replica_groups={{20,4,0,16,24,8,12,28},{21,5,1,17,25,9,13,29},{22,6,2,18,26,10,14,30},{..., dimensions={0} | all-to-all | bytes 393216 | tf_op jit(solution)/shard_map/all_to_all | solution.py:201
  20.9 0.0 copy-done
  20.9 0.0 copy-done.1
  20.9 0.0 copy-done.2
  20.9 0.0 copy-done.4
  20.9 1.7 %ffn.1 = bf16[8,8,1536]{2,1,0:T(8,128)(2,1)S(1)} custom-call(bf16[8,2048]{1,0:T(8,128)(2,1)S(1)} %bitcast.8, bf16[2048,768]{1,0:T(8,128)(2,1)S(1)} %bitcast.5, bf16[2048,768]{1,0:T(8,128)(2,1)S(1)} %bitcast.6, bf16[768,2048]{1,0:T(8,128)(2,1)S(1)} %bitcast.7, bf16[8,8,1536]{2,1,0:T(8,128)(2,1)S(1)} %all_to_all.16.x_ref), custom_call_target="tpu_custom_call" | custom-call | tf_op jit(solution)/shard_map/ffn/pallas_call | solution.py:139
  22.7 9.2 %all_to_all.17.y_ref = bf16[8,8,1536]{2,1,0:T(8,128)(2,1)S(1)} all-to-all(bf16[8,8,1536]{2,1,0:T(8,128)(2,1)S(1)} %ffn.1), channel_id=1, replica_groups={{20,4,0,16,24,8,12,28},{21,5,1,17,25,9,13,29},{22,6,2,18,26,10,14,30},{..., dimensions={0} | all-to-all | bytes 393216 | tf_op jit(solution)/shard_map/all_to_all | solution.py:201
  31.9 1.2 %combine.1 = bf16[256,2048]{1,0:T(8,128)(2,1)} custom-call(bf16[256,256]{1,0:T(8,128)(2,1)S(1)} %get-tuple-element.7.hot_ref, bf16[8,8,1536]{2,1,0:T(8,128)(2,1)S(1)} %all_to_all.17.y_ref), custom_call_target="tpu_custom_call" | custom-call | tf_op jit(solution)/shard_map/combine/pallas_call | solution.py:179
  (1 shorter events, 0.0 us)
Async XLA Ops:
  0.7 11.2 %copy-start.3 = (bf16[256,2048]{1,0:T(8,128)(2,1)S(1)}, bf16[256,2048]{1,0:T(8,128)(2,1)}, u32[]{:S(2)}) copy-start(bf16[256,2048]{1,0:T(8,128)(2,1)} %tokens_ref.1) | copy-start | bytes 3145732
  0.7 20.3 %copy-start = (bf16[1,2048,768]{2,1,0:T(8,128)(2,1)S(1)}, bf16[1,2048,768]{2,1,0:T(8,128)(2,1)}, u32[]{:S(2)}) copy-start(bf16[1,2048,768]{2,1,0:T(8,128)(2,1)} %param.8) | copy-start | bytes 9437188
  0.7 20.3 %copy-start.1 = (bf16[1,2048,768]{2,1,0:T(8,128)(2,1)S(1)}, bf16[1,2048,768]{2,1,0:T(8,128)(2,1)}, u32[]{:S(2)}) copy-start(bf16[1,2048,768]{2,1,0:T(8,128)(2,1)} %param.9) | copy-start | bytes 9437188
  0.7 20.3 %copy-start.2 = (bf16[1,768,2048]{2,1,0:T(8,128)(2,1)S(1)}, bf16[1,768,2048]{2,1,0:T(8,128)(2,1)}, u32[]{:S(2)}) copy-start(bf16[1,768,2048]{2,1,0:T(8,128)(2,1)} %param.10) | copy-start | bytes 9437188
  0.7 20.3 %copy-start.4 = (bf16[2048,8]{0,1:T(8,128)(2,1)S(1)}, bf16[2048,8]{0,1:T(8,128)(2,1)}, u32[]{:S(2)}) copy-start(bf16[2048,8]{0,1:T(8,128)(2,1)} %param.7) | copy-start | bytes 98308

commit v5 on v4

--- a/solution.py
+++ b/solution.py
@@ -55,7 +55,8 @@
         index = jnp.sum(jnp.where(place == wanted, value, 0), axis=2, keepdims=True) - 1
         hot = (index == column).astype(jnp.float32).reshape(n * slots, tok_dev)
         hots.append(hot.astype(jnp.bfloat16))
-        hot_ref[q * n * slots : (q + 1) * n * slots] = hots[q]
+        spot = (q + PARTS - 1) % PARTS * n * slots
+        hot_ref[spot : spot + n * slots] = hots[q]
     rows = n * slots
     tails = jnp.dot(
         jnp.concatenate(hots[1:], axis=0),
@@ -88,10 +89,9 @@
     )(table, tokens)
 
 
-def ffn_kernel(router_ref, gate_ref, up_ref, down_ref, x_ref, y_ref):
+def ffn_kernel(router_ref, gate_ref, up_ref, down_ref, hot_ref, x_ref, y_ref, turned_ref):
     n, slots, packed = x_ref.shape
     part = packed // (PARTS - 1)
-    width = part * PARTS
     rows = n * slots
     experts = router_ref.shape[0]
     me = lax.axis_index("dp").astype(jnp.int32)
@@ -125,29 +125,27 @@
     up_act = product(x, up_ref[...])
     silu = gate_act / (1.0 + jnp.exp(-gate_act))
     hidden = (gate_value * silu * up_act).astype(jnp.bfloat16)
-    y = product(hidden, down_ref[...])
-    y = y.reshape(n, slots, width)
-    last = y[:, :, packed:]
+    turned_ref[...] = hot_ref[...].T
+    last = product(hidden, down_ref[:, packed:]).reshape(n, slots, part)
     for q in range(PARTS - 1):
-        piece = y[:, :, q * part : (q + 1) * part]
+        piece = product(hidden, down_ref[:, q * part : (q + 1) * part]).reshape(n, slots, part)
         piece = jnp.where(row == MOST, last[:, q : q + 1], piece)
         piece = jnp.where(row == MOST + 1, last[:, q + THIRDS : q + THIRDS + 1], piece)
         y_ref[:, :, q * part : (q + 1) * part] = piece.astype(jnp.bfloat16)
 
 
-def ffn(router_t, w_gate, w_up, w_down, x):
+def ffn(router_t, w_gate, w_up, w_down, hots, x):
     return pl.pallas_call(
         ffn_kernel,
-        out_shape=jax.ShapeDtypeStruct(x.shape, jnp.bfloat16),
-        in_specs=[VMEM] * 5,
-        out_specs=VMEM,
+        out_shape=[
+            jax.ShapeDtypeStruct(x.shape, jnp.bfloat16),
+            jax.ShapeDtypeStruct(hots.shape[::-1], jnp.bfloat16),
+        ],
+        in_specs=[VMEM] * 6,
+        out_specs=[VMEM, VMEM],
         compiler_params=PARAMS,
         name="ffn",
-    )(router_t, w_gate, w_up, w_down, x)
-
-
-def place(hot, rows):
-    return lax.dot_general(hot, rows, (((0,), (0,)), ((), ())), preferred_element_type=jnp.float32)
+    )(router_t, w_gate, w_up, w_down, hots, x)
 
 
 def combine_kernel(hot_ref, y_ref, out_ref, block_ref, sem):
@@ -157,12 +155,15 @@
     copies = []
     pieces = [y_ref[:, :, q * part : (q + 1) * part] for q in range(PARTS - 1)]
     pieces = [p.astype(jnp.float32).reshape(rows, part).astype(jnp.bfloat16) for p in pieces]
-    head = hot_ref[:rows]
+    blank = jnp.zeros_like(pieces[0])
     for q in range(PARTS):
         if q < PARTS - 1:
-            total = place(head, pieces[q])
+            hot, values = hot_ref[:, 2 * rows :], [blank, pieces[q]]
         else:
-            total = place(hot_ref[rows:], jnp.concatenate(pieces, axis=0))
+            hot, values = hot_ref[...], pieces + [blank]
+        total = jnp.dot(
+            hot, jnp.concatenate(values, axis=0), preferred_element_type=jnp.float32
+        )
         block_ref[q] = total.astype(jnp.bfloat16)
         copy = pltpu.make_async_copy(
             block_ref.at[q], out_ref.at[:, pl.ds(q * part, part)], sem.at[q]
@@ -174,7 +175,7 @@
 
 
 def combine(hots, y):
-    tok_dev = hots.shape[1]
+    tok_dev = hots.shape[0]
     part = y.shape[2] // (PARTS - 1)
     return pl.pallas_call(
         combine_kernel,
@@ -212,8 +213,8 @@
     n = lax.axis_size("dp")
     send, hots = select(exchange(hold(jnp.broadcast_to(picks[None], (n,) + picks.shape))), tokens)
     received = exchange(send)
-    y = ffn(router.T, w_gate[0], w_up[0], w_down[0], received)
-    return combine(hots, exchange(y))
+    y, turned = ffn(router.T, w_gate[0], w_up[0], w_down[0], hots, received)
+    return combine(turned, exchange(y))
 
 
 def solution(mesh):

time: 33.3 us -> 33.3 us (level)
  no operation moved by 1% of the time
where the time goes in v5:
time: 33.3 us; the launch traced here: 33 us
  blocking collectives  28.9 us (87%)
  Pallas kernels  3.4 us (10%)
  local copies, waits for them, and re-layouts  0.68 us (2%)
    all_to_all x3, blocking collectives, exchange(): lax.all_to_all(value, 'dp', split_axis=0, concat_axis=0, tiled=True, axis...  28.9 us
    pallas_call x1, Pallas kernels, ffn(): pl.pallas_call(ffn_kernel, out_shape=[jax.ShapeDtypeStruct(x.shape, jnp.b...  1.73 us
    pallas_call x1, Pallas kernels, combine(): pl.pallas_call(combine_kernel, out_shape=jax.ShapeDtypeStruct((tok_dev, p...  1.21 us

profile of v5, /device:TPU:0, one launch (start us, length us, event | category | flops | bytes accessed | tf_op | source)
XLA Modules:
  0.0 33.0 jit_solution(18389392455510993954)
XLA Ops:
  0.0 0.7 %broadcast_in_dim.9.in_ref = s32[8,1,32]{2,1,0:T(1,128)S(1)} broadcast(s32[32]{0:T(128)} %bitcast.9), dimensions={2} | broadcast | bytes 1152 | tf_op jit(solution)/shard_map/broadcast_in_dim | solution.py:214
  0.7 0.0 copy-start.3
  0.7 0.0 copy-start
  0.7 0.0 copy-start.1
  0.7 0.0 copy-start.2
  0.7 0.0 copy-start.4
  0.7 11.1 %all_to_all.15.table_ref = s32[8,1,32]{2,1,0:T(1,128)S(1)} all-to-all(s32[8,1,32]{2,1,0:T(1,128)S(1)} %hold.1), channel_id=1, replica_groups={{20,4,0,16,24,8,12,28},{21,5,1,17,25,9,13,29},{22,6,2,18,26,10,14,30},{..., dimensions={0} | all-to-all | bytes 2048 | tf_op jit(solution)/shard_map/all_to_all | solution.py:202
  11.8 0.0 copy-done.3
  11.8 0.5 %select.1 = (bf16[8,8,1536]{2,1,0:T(8,128)(2,1)S(1)}, bf16[256,256]{1,0:T(8,128)(2,1)S(1)}) custom-call(s32[8,1,32]{2,1,0:T(1,128)S(1)} %all_to_all.15.table_ref, bf16[256,2048]{1,0:T(8,128)(2,1)S(1)} %copy-done.3), custom_call_target="tpu_custom_call" | custom-call | tf_op jit(solution)/shard_map/select/pallas_call | solution.py:79
  12.3 8.6 %all_to_all.16.x_ref = bf16[8,8,1536]{2,1,0:T(8,128)(2,1)S(1)} all-to-all(bf16[8,8,1536]{2,1,0:T(8,128)(2,1)S(1)} %get-tuple-element.10), channel_id=1, replica_groups={{20,4,0,16,24,8,12,28},{21,5,1,17,25,9,13,29},{22,6,2,18,26,10,14,30},{..., dimensions={0} | all-to-all | bytes 393216 | tf_op jit(solution)/shard_map/all_to_all | solution.py:202
  20.9 0.0 copy-done
  20.9 0.0 copy-done.1
  20.9 0.0 copy-done.2
  20.9 0.0 copy-done.4
  20.9 1.7 %ffn.1 = (bf16[8,8,1536]{2,1,0:T(8,128)(2,1)S(1)}, bf16[256,256]{1,0:T(8,128)(2,1)S(1)}) custom-call(bf16[8,2048]{1,0:T(8,128)(2,1)S(1)} %bitcast.8, bf16[2048,768]{1,0:T(8,128)(2,1)S(1)} %bitcast.5, bf16[2048,768]{1,0:T(8,128)(2,1)S(1)} %bitcast.6, bf16[768,2048]{1,0:T(8,128)(2,1)S(1)} %bitcast.7, bf16[256,256]{1,0:T(8,128)(2,1)S(1)} %get-tuple-element.9.hot_ref, ...), custom_call_target="tpu_custom_call" | custom-call | tf_op jit(solution)/shard_map/ffn/pallas_call | solution.py:138
  22.7 9.2 %all_to_all.17.y_ref = bf16[8,8,1536]{2,1,0:T(8,128)(2,1)S(1)} all-to-all(bf16[8,8,1536]{2,1,0:T(8,128)(2,1)S(1)} %get-tuple-element.12), channel_id=1, replica_groups={{20,4,0,16,24,8,12,28},{21,5,1,17,25,9,13,29},{22,6,2,18,26,10,14,30},{..., dimensions={0} | all-to-all | bytes 393216 | tf_op jit(solution)/shard_map/all_to_all | solution.py:202
  31.8 1.2 %combine.1 = bf16[256,2048]{1,0:T(8,128)(2,1)} custom-call(bf16[256,256]{1,0:T(8,128)(2,1)S(1)} %get-tuple-element.11.hot_ref, bf16[8,8,1536]{2,1,0:T(8,128)(2,1)S(1)} %all_to_all.17.y_ref), custom_call_target="tpu_custom_call" | custom-call | tf_op jit(solution)/shard_map/combine/pallas_call | solution.py:180
  (1 shorter events, 0.0 us)
Async XLA Ops:
  0.7 11.2 %copy-start.3 = (bf16[256,2048]{1,0:T(8,128)(2,1)S(1)}, bf16[256,2048]{1,0:T(8,128)(2,1)}, u32[]{:S(2)}) copy-start(bf16[256,2048]{1,0:T(8,128)(2,1)} %tokens_ref.1) | copy-start | bytes 3145732
  0.7 20.3 %copy-start = (bf16[1,2048,768]{2,1,0:T(8,128)(2,1)S(1)}, bf16[1,2048,768]{2,1,0:T(8,128)(2,1)}, u32[]{:S(2)}) copy-start(bf16[1,2048,768]{2,1,0:T(8,128)(2,1)} %param.8) | copy-start | bytes 9437188
  0.7 20.3 %copy-start.1 = (bf16[1,2048,768]{2,1,0:T(8,128)(2,1)S(1)}, bf16[1,2048,768]{2,1,0:T(8,128)(2,1)}, u32[]{:S(2)}) copy-start(bf16[1,2048,768]{2,1,0:T(8,128)(2,1)} %param.9) | copy-start | bytes 9437188
  0.7 20.3 %copy-start.2 = (bf16[1,768,2048]{2,1,0:T(8,128)(2,1)S(1)}, bf16[1,768,2048]{2,1,0:T(8,128)(2,1)}, u32[]{:S(2)}) copy-start(bf16[1,768,2048]{2,1,0:T(8,128)(2,1)} %param.10) | copy-start | bytes 9437188
  0.7 20.3 %copy-start.4 = (bf16[2048,8]{0,1:T(8,128)(2,1)S(1)}, bf16[2048,8]{0,1:T(8,128)(2,1)}, u32[]{:S(2)}) copy-start(bf16[2048,8]{0,1:T(8,128)(2,1)} %param.7) | copy-start | bytes 98308

commit v6 on v5

--- a/solution.py
+++ b/solution.py
@@ -33,8 +33,8 @@
 
 def select_kernel(table_ref, tokens_ref, send_ref, hot_ref):
     tok_dev, width = tokens_ref.shape
-    n, slots, _ = send_ref.shape
-    capacity = table_ref.shape[2]
+    n, _, capacity = table_ref.shape
+    slots = SLOTS
     part = width // PARTS
     me = lax.axis_index("dp").astype(jnp.int32)
     table = jnp.broadcast_to(table_ref[...], (n, slots, capacity))
@@ -68,9 +68,7 @@
             hots[0], tokens_ref[:, q * part : (q + 1) * part], preferred_element_type=jnp.float32
         )
         chosen = chosen + tails[q * rows : (q + 1) * rows]
-        send_ref[:, :, q * part : (q + 1) * part] = chosen.reshape(n, slots, part).astype(
-            jnp.bfloat16
-        )
+        send_ref[:, q * part : (q + 1) * part] = chosen.astype(jnp.bfloat16)
 
 
 def select(table, tokens):
@@ -79,7 +77,7 @@
     return pl.pallas_call(
         select_kernel,
         out_shape=[
-            jax.ShapeDtypeStruct((n, SLOTS, width // PARTS * (PARTS - 1)), jnp.bfloat16),
+            jax.ShapeDtypeStruct((n * SLOTS, width // PARTS * (PARTS - 1)), jnp.bfloat16),
             jax.ShapeDtypeStruct((PARTS * n * SLOTS, tok_dev), jnp.bfloat16),
         ],
         in_specs=[VMEM, VMEM],
@@ -90,20 +88,18 @@
 
 
 def ffn_kernel(router_ref, gate_ref, up_ref, down_ref, hot_ref, x_ref, y_ref, turned_ref):
-    n, slots, packed = x_ref.shape
+    rows, packed = x_ref.shape
     part = packed // (PARTS - 1)
-    rows = n * slots
+    n, slots = rows // SLOTS, SLOTS
     experts = router_ref.shape[0]
     me = lax.axis_index("dp").astype(jnp.int32)
-    head = x_ref[...].astype(jnp.float32)
     row = lax.broadcasted_iota(jnp.int32, (n, slots, part), 1)
     tail = jnp.zeros((n, slots, part), jnp.float32)
     for q in range(PARTS - 1):
-        piece = head[:, :, q * part : (q + 1) * part]
+        piece = x_ref[:, q * part : (q + 1) * part].astype(jnp.float32).reshape(n, slots, part)
         tail = jnp.where(row == q, piece[:, MOST : MOST + 1], tail)
         tail = jnp.where(row == q + THIRDS, piece[:, MOST + 1 : MOST + 2], tail)
-    x = jnp.concatenate([head.reshape(rows, packed), tail.reshape(rows, part)], axis=1)
-    x = x.astype(jnp.bfloat16)
+    x = jnp.concatenate([x_ref[...], tail.reshape(rows, part).astype(jnp.bfloat16)], axis=1)
     logits = lax.dot_general(
         x, router_ref[...], (((1,), (1,)), ((), ())), preferred_element_type=jnp.float32
     )
@@ -131,7 +127,7 @@
         piece = product(hidden, down_ref[:, q * part : (q + 1) * part]).reshape(n, slots, part)
         piece = jnp.where(row == MOST, last[:, q : q + 1], piece)
         piece = jnp.where(row == MOST + 1, last[:, q + THIRDS : q + THIRDS + 1], piece)
-        y_ref[:, :, q * part : (q + 1) * part] = piece.astype(jnp.bfloat16)
+        y_ref[:, q * part : (q + 1) * part] = piece.reshape(rows, part).astype(jnp.bfloat16)
 
 
 def ffn(router_t, w_gate, w_up, w_down, hots, x):
@@ -149,12 +145,10 @@
 
 
 def combine_kernel(hot_ref, y_ref, out_ref, block_ref, sem):
-    n, slots, packed = y_ref.shape
+    rows, packed = y_ref.shape
     part = packed // (PARTS - 1)
-    rows = n * slots
     copies = []
-    pieces = [y_ref[:, :, q * part : (q + 1) * part] for q in range(PARTS - 1)]
-    pieces = [p.astype(jnp.float32).reshape(rows, part).astype(jnp.bfloat16) for p in pieces]
+    pieces = [y_ref[:, q * part : (q + 1) * part] for q in range(PARTS - 1)]
     blank = jnp.zeros_like(pieces[0])
     for q in range(PARTS):
         if q < PARTS - 1:
@@ -176,7 +170,7 @@
 
 def combine(hots, y):
     tok_dev = hots.shape[0]
-    part = y.shape[2] // (PARTS - 1)
+    part = y.shape[1] // (PARTS - 1)
     return pl.pallas_call(
         combine_kernel,
         out_shape=jax.ShapeDtypeStruct((tok_dev, part * PARTS), jnp.bfloat16),
@@ -209,12 +203,17 @@
     )
 
 
+def swap(rows, n):
+    return exchange(rows.reshape(n, SLOTS, rows.shape[1])).reshape(rows.shape)
+
+
 def body(tokens, router, w_gate, w_up, w_down, picks):
     n = lax.axis_size("dp")
-    send, hots = select(exchange(hold(jnp.broadcast_to(picks[None], (n,) + picks.shape))), tokens)
-    received = exchange(send)
+    table = exchange(hold(jnp.broadcast_to(picks[None], (n,) + picks.shape)))
+    send, hots = select(table, tokens)
+    received = swap(send, n)
     y, turned = ffn(router.T, w_gate[0], w_up[0], w_down[0], hots, received)
-    return combine(turned, exchange(y))
+    return combine(turned, swap(y, n))
 
 
 def solution(mesh):

time: 33.3 us -> 33.3 us (level)
  no operation moved by 1% of the time
where the time goes in v6:
time: 33.3 us; the launch traced here: 33 us
  blocking collectives  28.9 us (87%)
  Pallas kernels  3.39 us (10%)
  local copies, waits for them, and re-layouts  0.68 us (2%)
    all_to_all x3, blocking collectives, exchange(): lax.all_to_all(value, 'dp', split_axis=0, concat_axis=0, tiled=True, axis...  28.9 us
    pallas_call x1, Pallas kernels, ffn(): pl.pallas_call(ffn_kernel, out_shape=[jax.ShapeDtypeStruct(x.shape, jnp.b...  1.73 us
    pallas_call x1, Pallas kernels, combine(): pl.pallas_call(combine_kernel, out_shape=jax.ShapeDtypeStruct((tok_dev, p...  1.21 us

profile of v6, /device:TPU:0, one launch (start us, length us, event | category | flops | bytes accessed | tf_op | source)
XLA Modules:
  0.0 33.0 jit_solution(14759949303068366074)
XLA Ops:
  0.0 0.7 %broadcast_in_dim.9.in_ref = s32[8,1,32]{2,1,0:T(1,128)S(1)} broadcast(s32[32]{0:T(128)} %bitcast.17), dimensions={2} | broadcast | bytes 1152 | tf_op jit(solution)/shard_map/broadcast_in_dim | solution.py:212
  0.7 0.0 copy-start.3
  0.7 0.0 copy-start
  0.7 0.0 copy-start.1
  0.7 0.0 copy-start.2
  0.7 0.0 copy-start.4
  0.7 11.1 %all_to_all.15.table_ref = s32[8,1,32]{2,1,0:T(1,128)S(1)} all-to-all(s32[8,1,32]{2,1,0:T(1,128)S(1)} %hold.1), channel_id=1, replica_groups={{20,4,0,16,24,8,12,28},{21,5,1,17,25,9,13,29},{22,6,2,18,26,10,14,30},{..., dimensions={0} | all-to-all | bytes 2048 | tf_op jit(solution)/shard_map/all_to_all | solution.py:196
  11.8 0.0 copy-done.3
  11.8 0.5 %select.1 = (bf16[64,1536]{1,0:T(8,128)(2,1)S(1)}, bf16[256,256]{1,0:T(8,128)(2,1)S(1)}) custom-call(s32[8,1,32]{2,1,0:T(1,128)S(1)} %all_to_all.15.table_ref, bf16[256,2048]{1,0:T(8,128)(2,1)S(1)} %copy-done.3), custom_call_target="tpu_custom_call" | custom-call | tf_op jit(solution)/shard_map/select/pallas_call | solution.py:77
  12.3 8.6 %all_to_all.16 = bf16[8,8,1536]{2,1,0:T(8,128)(2,1)S(1)} all-to-all(bf16[8,8,1536]{2,1,0:T(8,128)(2,1)S(1)} %bitcast.15), channel_id=1, replica_groups={{20,4,0,16,24,8,12,28},{21,5,1,17,25,9,13,29},{22,6,2,18,26,10,14,30},{..., dimensions={0} | all-to-all | bytes 393216 | tf_op jit(solution)/shard_map/all_to_all | solution.py:196
  20.9 0.0 copy-done
  20.9 0.0 copy-done.1
  20.9 0.0 copy-done.2
  20.9 0.0 copy-done.4
  20.9 1.7 %ffn.1 = (bf16[64,1536]{1,0:T(8,128)(2,1)S(1)}, bf16[256,256]{1,0:T(8,128)(2,1)S(1)}) custom-call(bf16[8,2048]{1,0:T(8,128)(2,1)S(1)} %bitcast.16, bf16[2048,768]{1,0:T(8,128)(2,1)S(1)} %bitcast.9, bf16[2048,768]{1,0:T(8,128)(2,1)S(1)} %bitcast.10, bf16[768,2048]{1,0:T(8,128)(2,1)S(1)} %bitcast.11, bf16[256,256]{1,0:T(8,128)(2,1)S(1)} %get-tuple-element.9.hot_ref, ...), custom_call_target="tpu_custom_call" | custom-call | tf_op jit(solution)/shard_map/ffn/pallas_call | solution.py:134
  22.7 9.2 %all_to_all.17 = bf16[8,8,1536]{2,1,0:T(8,128)(2,1)S(1)} all-to-all(bf16[8,8,1536]{2,1,0:T(8,128)(2,1)S(1)} %bitcast.14), channel_id=1, replica_groups={{20,4,0,16,24,8,12,28},{21,5,1,17,25,9,13,29},{22,6,2,18,26,10,14,30},{..., dimensions={0} | all-to-all | bytes 393216 | tf_op jit(solution)/shard_map/all_to_all | solution.py:196
  31.8 1.2 %combine.1 = bf16[256,2048]{1,0:T(8,128)(2,1)} custom-call(bf16[256,256]{1,0:T(8,128)(2,1)S(1)} %get-tuple-element.11.hot_ref, bf16[64,1536]{1,0:T(8,128)(2,1)S(1)} %bitcast.12), custom_call_target="tpu_custom_call" | custom-call | tf_op jit(solution)/shard_map/combine/pallas_call | solution.py:174
  (1 shorter events, 0.0 us)
Async XLA Ops:
  0.7 11.2 %copy-start.3 = (bf16[256,2048]{1,0:T(8,128)(2,1)S(1)}, bf16[256,2048]{1,0:T(8,128)(2,1)}, u32[]{:S(2)}) copy-start(bf16[256,2048]{1,0:T(8,128)(2,1)} %tokens_ref.1) | copy-start | bytes 3145732
  0.7 20.3 %copy-start = (bf16[1,2048,768]{2,1,0:T(8,128)(2,1)S(1)}, bf16[1,2048,768]{2,1,0:T(8,128)(2,1)}, u32[]{:S(2)}) copy-start(bf16[1,2048,768]{2,1,0:T(8,128)(2,1)} %param.8) | copy-start | bytes 9437188
  0.7 20.3 %copy-start.1 = (bf16[1,2048,768]{2,1,0:T(8,128)(2,1)S(1)}, bf16[1,2048,768]{2,1,0:T(8,128)(2,1)}, u32[]{:S(2)}) copy-start(bf16[1,2048,768]{2,1,0:T(8,128)(2,1)} %param.9) | copy-start | bytes 9437188
  0.7 20.3 %copy-start.2 = (bf16[1,768,2048]{2,1,0:T(8,128)(2,1)S(1)}, bf16[1,768,2048]{2,1,0:T(8,128)(2,1)}, u32[]{:S(2)}) copy-start(bf16[1,768,2048]{2,1,0:T(8,128)(2,1)} %param.10) | copy-start | bytes 9437188
  0.7 20.3 %copy-start.4 = (bf16[2048,8]{0,1:T(8,128)(2,1)S(1)}, bf16[2048,8]{0,1:T(8,128)(2,1)}, u32[]{:S(2)}) copy-start(bf16[2048,8]{0,1:T(8,128)(2,1)} %param.7) | copy-start | bytes 98308

commit v7 on v6

--- a/solution.py
+++ b/solution.py
@@ -15,20 +15,24 @@
 PARAMS = pltpu.CompilerParams(vmem_limit_bytes=16 * 1024 * 1024)
 
 
-def hold_kernel(in_ref, out_ref):
-    out_ref[...] = in_ref[...]
-
-
-def hold(value):
+def hold_kernel(picks_ref, out_ref, row_ref, sem):
+    copy = pltpu.make_async_copy(picks_ref, row_ref, sem)
+    copy.start()
+    copy.wait()
+    out_ref[...] = jnp.broadcast_to(row_ref[...][None], out_ref.shape)
+
+
+def hold(picks, n):
     return pl.pallas_call(
         hold_kernel,
-        out_shape=jax.ShapeDtypeStruct(value.shape, value.dtype),
-        in_specs=[VMEM],
+        out_shape=jax.ShapeDtypeStruct((n,) + picks.shape, picks.dtype),
+        in_specs=[pl.BlockSpec(memory_space=pltpu.HBM)],
         out_specs=VMEM,
+        scratch_shapes=[pltpu.VMEM(picks.shape, picks.dtype), pltpu.SemaphoreType.DMA],
         compiler_params=PARAMS,
         cost_estimate=pl.CostEstimate(flops=LONG, bytes_accessed=0, transcendentals=0),
         name="hold",
-    )(value)
+    )(picks)
 
 
 def select_kernel(table_ref, tokens_ref, send_ref, hot_ref):
@@ -209,7 +213,7 @@
 
 def body(tokens, router, w_gate, w_up, w_down, picks):
     n = lax.axis_size("dp")
-    table = exchange(hold(jnp.broadcast_to(picks[None], (n,) + picks.shape)))
+    table = exchange(hold(picks, n))
     send, hots = select(table, tokens)
     received = swap(send, n)
     y, turned = ffn(router.T, w_gate[0], w_up[0], w_down[0], hots, received)

time: 33.3 us -> 33.3 us (level)
    unnamed x10 -> x12, local copies, waits for them, and re-layouts: 0.02 us -> 0.76 us
    broadcast_in_dim x1 -> x0, local copies, waits for them, and re-layouts: 0.66 us -> none  [body(): table = exchange(hold(jnp.broadcast_to(picks[None], (n,) + picks.shape)))]
where the time goes in v7:
time: 33.3 us; the launch traced here: 33.1 us
  blocking collectives  28.9 us (87%)
  Pallas kernels  3.41 us (10%)
  local copies, waits for them, and re-layouts  0.76 us (2%)
    all_to_all x3, blocking collectives, exchange(): lax.all_to_all(value, 'dp', split_axis=0, concat_axis=0, tiled=True, axis...  28.9 us
    pallas_call x1, Pallas kernels, ffn(): pl.pallas_call(ffn_kernel, out_shape=[jax.ShapeDtypeStruct(x.shape, jnp.b...  1.73 us
    pallas_call x1, Pallas kernels, combine(): pl.pallas_call(combine_kernel, out_shape=jax.ShapeDtypeStruct((tok_dev, p...  1.21 us
    unnamed x12, local copies, waits for them, and re-layouts  0.76 us

profile of v7, /device:TPU:0, one launch (start us, length us, event | category | flops | bytes accessed | tf_op | source)
XLA Modules:
  0.0 33.1 jit_solution(9561056671586859117)
XLA Ops:
  0.0 0.0 copy-start.3
  0.0 0.0 copy-start.5
  0.0 0.7 %copy-done.5 = s32[1,32]{1,0:T(1,128)S(1)} copy-done((s32[1,32]{1,0:T(1,128)S(1)}, s32[1,32]{1,0:T(1,128)}, u32[]{:S(2)}) %copy-start.5) | copy-done | bytes 152
  0.7 0.0 copy-start
  0.7 0.0 copy-start.1
  0.8 0.0 copy-start.2
  0.8 0.0 copy-start.4
  0.8 11.1 %all_to_all.15.table_ref = s32[8,1,32]{2,1,0:T(1,128)S(1)} all-to-all(s32[8,1,32]{2,1,0:T(1,128)S(1)} %hold.1), channel_id=1, replica_groups={{20,4,0,16,24,8,12,28},{21,5,1,17,25,9,13,29},{22,6,2,18,26,10,14,30},{..., dimensions={0} | all-to-all | bytes 2048 | tf_op jit(solution)/shard_map/all_to_all | solution.py:200
  11.9 0.0 copy-done.3
  11.9 0.5 %select.1 = (bf16[64,1536]{1,0:T(8,128)(2,1)S(1)}, bf16[256,256]{1,0:T(8,128)(2,1)S(1)}) custom-call(s32[8,1,32]{2,1,0:T(1,128)S(1)} %all_to_all.15.table_ref, bf16[256,2048]{1,0:T(8,128)(2,1)S(1)} %copy-done.3), custom_call_target="tpu_custom_call" | custom-call | tf_op jit(solution)/shard_map/select/pallas_call | solution.py:81
  12.4 8.6 %all_to_all.16 = bf16[8,8,1536]{2,1,0:T(8,128)(2,1)S(1)} all-to-all(bf16[8,8,1536]{2,1,0:T(8,128)(2,1)S(1)} %bitcast.14), channel_id=1, replica_groups={{20,4,0,16,24,8,12,28},{21,5,1,17,25,9,13,29},{22,6,2,18,26,10,14,30},{..., dimensions={0} | all-to-all | bytes 393216 | tf_op jit(solution)/shard_map/all_to_all | solution.py:200
  21.0 0.0 copy-done
  21.0 0.0 copy-done.1
  21.0 0.0 copy-done.2
  21.0 0.0 copy-done.4
  21.0 1.7 %ffn.1 = (bf16[64,1536]{1,0:T(8,128)(2,1)S(1)}, bf16[256,256]{1,0:T(8,128)(2,1)S(1)}) custom-call(bf16[8,2048]{1,0:T(8,128)(2,1)S(1)} %bitcast.15, bf16[2048,768]{1,0:T(8,128)(2,1)S(1)} %bitcast.8, bf16[2048,768]{1,0:T(8,128)(2,1)S(1)} %bitcast.9, bf16[768,2048]{1,0:T(8,128)(2,1)S(1)} %bitcast.10, bf16[256,256]{1,0:T(8,128)(2,1)S(1)} %get-tuple-element.9.hot_ref, ...), custom_call_target="tpu_custom_call" | custom-call | tf_op jit(solution)/shard_map/ffn/pallas_call | solution.py:138
  22.8 9.2 %all_to_all.17 = bf16[8,8,1536]{2,1,0:T(8,128)(2,1)S(1)} all-to-all(bf16[8,8,1536]{2,1,0:T(8,128)(2,1)S(1)} %bitcast.13), channel_id=1, replica_groups={{20,4,0,16,24,8,12,28},{21,5,1,17,25,9,13,29},{22,6,2,18,26,10,14,30},{..., dimensions={0} | all-to-all | bytes 393216 | tf_op jit(solution)/shard_map/all_to_all | solution.py:200
  31.9 1.2 %combine.1 = bf16[256,2048]{1,0:T(8,128)(2,1)} custom-call(bf16[256,256]{1,0:T(8,128)(2,1)S(1)} %get-tuple-element.11.hot_ref, bf16[64,1536]{1,0:T(8,128)(2,1)S(1)} %bitcast.11), custom_call_target="tpu_custom_call" | custom-call | tf_op jit(solution)/shard_map/combine/pallas_call | solution.py:178
  (1 shorter events, 0.0 us)
Async XLA Ops:
  0.0 11.9 %copy-start.3 = (bf16[256,2048]{1,0:T(8,128)(2,1)S(1)}, bf16[256,2048]{1,0:T(8,128)(2,1)}, u32[]{:S(2)}) copy-start(bf16[256,2048]{1,0:T(8,128)(2,1)} %tokens_ref.1) | copy-start | bytes 3145732
  0.0 0.7 %copy-start.5 = (s32[1,32]{1,0:T(1,128)S(1)}, s32[1,32]{1,0:T(1,128)}, u32[]{:S(2)}) copy-start(s32[1,32]{1,0:T(1,128)} %picks_ref.1) | copy-start | bytes 388
  0.7 20.3 %copy-start = (bf16[1,2048,768]{2,1,0:T(8,128)(2,1)S(1)}, bf16[1,2048,768]{2,1,0:T(8,128)(2,1)}, u32[]{:S(2)}) copy-start(bf16[1,2048,768]{2,1,0:T(8,128)(2,1)} %param.8) | copy-start | bytes 9437188
  0.7 20.3 %copy-start.1 = (bf16[1,2048,768]{2,1,0:T(8,128)(2,1)S(1)}, bf16[1,2048,768]{2,1,0:T(8,128)(2,1)}, u32[]{:S(2)}) copy-start(bf16[1,2048,768]{2,1,0:T(8,128)(2,1)} %param.9) | copy-start | bytes 9437188
  0.8 20.3 %copy-start.2 = (bf16[1,768,2048]{2,1,0:T(8,128)(2,1)S(1)}, bf16[1,768,2048]{2,1,0:T(8,128)(2,1)}, u32[]{:S(2)}) copy-start(bf16[1,768,2048]{2,1,0:T(8,128)(2,1)} %param.10) | copy-start | bytes 9437188
  0.8 20.3 %copy-start.4 = (bf16[2048,8]{0,1:T(8,128)(2,1)S(1)}, bf16[2048,8]{0,1:T(8,128)(2,1)}, u32[]{:S(2)}) copy-start(bf16[2048,8]{0,1:T(8,128)(2,1)} %param.7) | copy-start | bytes 98308

commit v8 on v6

--- a/solution.py
+++ b/solution.py
@@ -41,7 +41,8 @@
     local = table - me * tok_dev
     row = lax.broadcasted_iota(jnp.int32, local.shape, 1)
     lane = lax.broadcasted_iota(jnp.int32, local.shape, 2)
-    column = lax.broadcasted_iota(jnp.int32, (n, slots, tok_dev), 2)
+    column = lax.broadcasted_iota(jnp.int32, (n * slots, tok_dev), 1).astype(jnp.int16)
+    one, zero = jnp.bfloat16(1), jnp.bfloat16(0)
     start = jnp.sum((local < 0).astype(jnp.int32), axis=2, keepdims=True)
     place = lane - start
     value = jnp.where((local >= 0) & (local < tok_dev), local + 1, 0)
@@ -53,8 +54,12 @@
             first, second = q - 1, q - 1 + THIRDS
             wanted = jnp.where(row == MOST, first, jnp.where(row == MOST + 1, second, -1))
         index = jnp.sum(jnp.where(place == wanted, value, 0), axis=2, keepdims=True) - 1
-        hot = (index == column).astype(jnp.float32).reshape(n * slots, tok_dev)
-        hots.append(hot.astype(jnp.bfloat16))
+        spread = jnp.broadcast_to(index, (n, slots, 128)).reshape(n * slots, 128).astype(jnp.int16)
+        hot = [
+            jnp.where(spread == column[:, c : c + 128], one, zero)
+            for c in range(0, tok_dev, 128)
+        ]
+        hots.append(jnp.concatenate(hot, axis=1))
         spot = (q + PARTS - 1) % PARTS * n * slots
         hot_ref[spot : spot + n * slots] = hots[q]
     rows = n * slots

time: 33.3 us -> 33.3 us (level)
  no operation moved by 1% of the time
where the time goes in v8:
time: 33.3 us; the launch traced here: 33 us
  blocking collectives  28.9 us (87%)
  Pallas kernels  3.39 us (10%)
  local copies, waits for them, and re-layouts  0.68 us (2%)
    all_to_all x3, blocking collectives, exchange(): lax.all_to_all(value, 'dp', split_axis=0, concat_axis=0, tiled=True, axis...  28.9 us
    pallas_call x1, Pallas kernels, ffn(): pl.pallas_call(ffn_kernel, out_shape=[jax.ShapeDtypeStruct(x.shape, jnp.b...  1.73 us
    pallas_call x1, Pallas kernels, combine(): pl.pallas_call(combine_kernel, out_shape=jax.ShapeDtypeStruct((tok_dev, p...  1.21 us

profile of v8, /device:TPU:0, one launch (start us, length us, event | category | flops | bytes accessed | tf_op | source)
XLA Modules:
  0.0 33.0 jit_solution(14299084561323473355)
XLA Ops:
  0.0 0.7 %broadcast_in_dim.9.in_ref = s32[8,1,32]{2,1,0:T(1,128)S(1)} broadcast(s32[32]{0:T(128)} %bitcast.17), dimensions={2} | broadcast | bytes 1152 | tf_op jit(solution)/shard_map/broadcast_in_dim | solution.py:217
  0.7 0.0 copy-start.3
  0.7 0.0 copy-start
  0.7 0.0 copy-start.1
  0.7 0.0 copy-start.2
  0.7 0.0 copy-start.4
  0.7 11.1 %all_to_all.15.table_ref = s32[8,1,32]{2,1,0:T(1,128)S(1)} all-to-all(s32[8,1,32]{2,1,0:T(1,128)S(1)} %hold.1), channel_id=1, replica_groups={{20,4,0,16,24,8,12,28},{21,5,1,17,25,9,13,29},{22,6,2,18,26,10,14,30},{..., dimensions={0} | all-to-all | bytes 2048 | tf_op jit(solution)/shard_map/all_to_all | solution.py:201
  11.8 0.0 copy-done.3
  11.8 0.5 %select.1 = (bf16[64,1536]{1,0:T(8,128)(2,1)S(1)}, bf16[256,256]{1,0:T(8,128)(2,1)S(1)}) custom-call(s32[8,1,32]{2,1,0:T(1,128)S(1)} %all_to_all.15.table_ref, bf16[256,2048]{1,0:T(8,128)(2,1)S(1)} %copy-done.3), custom_call_target="tpu_custom_call" | custom-call | tf_op jit(solution)/shard_map/select/pallas_call | solution.py:82
  12.3 8.6 %all_to_all.16 = bf16[8,8,1536]{2,1,0:T(8,128)(2,1)S(1)} all-to-all(bf16[8,8,1536]{2,1,0:T(8,128)(2,1)S(1)} %bitcast.15), channel_id=1, replica_groups={{20,4,0,16,24,8,12,28},{21,5,1,17,25,9,13,29},{22,6,2,18,26,10,14,30},{..., dimensions={0} | all-to-all | bytes 393216 | tf_op jit(solution)/shard_map/all_to_all | solution.py:201
  20.9 0.0 copy-done
  20.9 0.0 copy-done.1
  20.9 0.0 copy-done.2
  20.9 0.0 copy-done.4
  20.9 1.7 %ffn.1 = (bf16[64,1536]{1,0:T(8,128)(2,1)S(1)}, bf16[256,256]{1,0:T(8,128)(2,1)S(1)}) custom-call(bf16[8,2048]{1,0:T(8,128)(2,1)S(1)} %bitcast.16, bf16[2048,768]{1,0:T(8,128)(2,1)S(1)} %bitcast.9, bf16[2048,768]{1,0:T(8,128)(2,1)S(1)} %bitcast.10, bf16[768,2048]{1,0:T(8,128)(2,1)S(1)} %bitcast.11, bf16[256,256]{1,0:T(8,128)(2,1)S(1)} %get-tuple-element.9.hot_ref, ...), custom_call_target="tpu_custom_call" | custom-call | tf_op jit(solution)/shard_map/ffn/pallas_call | solution.py:139
  22.7 9.2 %all_to_all.17 = bf16[8,8,1536]{2,1,0:T(8,128)(2,1)S(1)} all-to-all(bf16[8,8,1536]{2,1,0:T(8,128)(2,1)S(1)} %bitcast.14), channel_id=1, replica_groups={{20,4,0,16,24,8,12,28},{21,5,1,17,25,9,13,29},{22,6,2,18,26,10,14,30},{..., dimensions={0} | all-to-all | bytes 393216 | tf_op jit(solution)/shard_map/all_to_all | solution.py:201
  31.8 1.2 %combine.1 = bf16[256,2048]{1,0:T(8,128)(2,1)} custom-call(bf16[256,256]{1,0:T(8,128)(2,1)S(1)} %get-tuple-element.11.hot_ref, bf16[64,1536]{1,0:T(8,128)(2,1)S(1)} %bitcast.12), custom_call_target="tpu_custom_call" | custom-call | tf_op jit(solution)/shard_map/combine/pallas_call | solution.py:179
  (1 shorter events, 0.0 us)
Async XLA Ops:
  0.7 11.2 %copy-start.3 = (bf16[256,2048]{1,0:T(8,128)(2,1)S(1)}, bf16[256,2048]{1,0:T(8,128)(2,1)}, u32[]{:S(2)}) copy-start(bf16[256,2048]{1,0:T(8,128)(2,1)} %tokens_ref.1) | copy-start | bytes 3145732
  0.7 20.3 %copy-start = (bf16[1,2048,768]{2,1,0:T(8,128)(2,1)S(1)}, bf16[1,2048,768]{2,1,0:T(8,128)(2,1)}, u32[]{:S(2)}) copy-start(bf16[1,2048,768]{2,1,0:T(8,128)(2,1)} %param.8) | copy-start | bytes 9437188
  0.7 20.3 %copy-start.1 = (bf16[1,2048,768]{2,1,0:T(8,128)(2,1)S(1)}, bf16[1,2048,768]{2,1,0:T(8,128)(2,1)}, u32[]{:S(2)}) copy-start(bf16[1,2048,768]{2,1,0:T(8,128)(2,1)} %param.9) | copy-start | bytes 9437188
  0.7 20.3 %copy-start.2 = (bf16[1,768,2048]{2,1,0:T(8,128)(2,1)S(1)}, bf16[1,768,2048]{2,1,0:T(8,128)(2,1)}, u32[]{:S(2)}) copy-start(bf16[1,768,2048]{2,1,0:T(8,128)(2,1)} %param.10) | copy-start | bytes 9437188
  0.7 20.3 %copy-start.4 = (bf16[2048,8]{0,1:T(8,128)(2,1)S(1)}, bf16[2048,8]{0,1:T(8,128)(2,1)}, u32[]{:S(2)}) copy-start(bf16[2048,8]{0,1:T(8,128)(2,1)} %param.7) | copy-start | bytes 98308
